TPU v7x, 32 devices: a whole 2x2x4 slice. The times are simulated.
32 devices in a mesh: dp: 4 (over z), row: 2 (over x), col: 4 (over y, core).
Axes of the slice: x: 2, y: 2, z: 4, core: 2. Of those that a mesh axis runs over, the one named last changes fastest.
Arguments:
- inputs: float32 [8192, 1024], P(('dp', 'row'), 'col'), may hold values from -6 to 6
- cond: float32 [8, 1024], P(('dp', 'row')), may hold values from -10 to 10
- w_ada: bfloat16 [1024, 6, 1024], P(None, None, 'col'), may hold values from -0.1875 to 0.1875
- b_ada: float32 [6, 1024], P(None, 'col'), may hold values from -3 to 3
- w_qkv: bfloat16 [3, 1024, 1024], P(None, 'col', 'row'), may hold values from -0.1875 to 0.1875
- b_qv: float32 [2, 1024], P(None, ('row', 'col')), may hold values from -3 to 3
- w_out: bfloat16 [1024, 1024], P('row', 'col'), may hold values from -0.75 to 0.75
- b_out: float32 [1024], P('col'), may hold values from -3 to 3
- w_fc1: bfloat16 [1024, 4096], P('col', 'row'), may hold values from -0.1875 to 0.1875
- b_fc1: float32 [4096], P(('row', 'col')), may hold values from -3 to 3
- w_fc2: bfloat16 [4096, 1024], P('row', 'col'), may hold values from -0.09375 to 0.09375
- b_fc2: float32 [1024], P('col'), may hold values from -5 to 5
- cotangent: float32 [8192, 1024], P(('dp', 'row'), 'col'), may hold values from -6 to 6
Outputs:
- result: float32 [8192, 1024], P(('dp', 'row'), 'col')
- grad_inputs: float32 [8192, 1024], P(('dp', 'row'), 'col')
- grad_cond: float32 [8, 1024], P(('dp', 'row'))
- grad_w_ada: float32 [1024, 6, 1024], P(None, None, 'col')
- grad_b_ada: float32 [6, 1024], P(None, 'col')
- gradient_query_key_value_weight: float32 [3, 1024, 1024], P(None, 'col', 'row')
- gradient_query_value_bias: float32 [2, 1024], P(None, ('row', 'col'))
- gradient_output_weight: float32 [1024, 1024], P('row', 'col')
- gradient_output_bias: float32 [1024], P('col')
- gradient_first_dense_weight: float32 [1024, 4096], P('col', 'row')
- gradient_first_dense_bias: float32 [4096], P(('row', 'col'))
- gradient_second_dense_weight: float32 [4096, 1024], P('row', 'col')
- gradient_second_dense_bias: float32 [1024], P('col')
All inputs are finite; a program needn't handle non-finite values.
Results may differ from a plain program's by a relative error of at most 0.0131.
The roundings to bfloat16 on the way count: a program that leaves them out, or rounds other values in their place, can miss the bound.
Values may be sent and summed in bfloat16 or wider, within the bound.
A program may use at most 192 MiB of HBM per device.

v0:
```python
import jax
import jax.numpy as jnp
from jax import lax
from jax.sharding import PartitionSpec as P

D = 1024
HD = 64
LATENT_TOKENS = 1024


EPSILON = 1e-06


def gelu_tanh(values):
    return jax.nn.gelu(values, approximate=True)


def norm_stats(fields):
    sums_one, sums_two = lax.psum(
        (jnp.sum(fields, axis=-1), jnp.sum(fields * fields, axis=-1)), "col"
    )
    average = sums_one / D
    inverse = lax.rsqrt(sums_two / D - average * average + EPSILON)
    return ((fields - average[..., None]) * inverse[..., None], inverse)


def norm_back(grad_norm, normed, inverse):
    sums_one, sums_two = lax.psum(
        (jnp.sum(grad_norm, axis=-1), jnp.sum(grad_norm * normed, axis=-1)), "col"
    )
    return inverse[..., None] * (
        grad_norm - sums_one[..., None] / D - normed * sums_two[..., None] / D
    )


def rows_forward(local):
    return lax.all_gather(local, "row", axis=0, tiled=True)


def cols_forward(local):
    return lax.all_gather(local, "col", axis=1, tiled=True)


def cols_forward_sum(partial_value):
    return lax.psum_scatter(partial_value, "col", scatter_dimension=2, tiled=True)


def rows_forward_sum(partial_value):
    return lax.psum_scatter(partial_value, "row", scatter_dimension=0, tiled=True)


def rows_backward(local):
    return lax.all_gather(local, "row", axis=0, tiled=True)


def cols_backward(local):
    return lax.all_gather(local, "col", axis=2, tiled=True)


def cols_backward_sum(partial_value):
    return lax.psum_scatter(partial_value, "col", scatter_dimension=1, tiled=True)


def rows_backward_sum(partial_value):
    return lax.psum_scatter(partial_value, "row", scatter_dimension=0, tiled=True)


def attend(packed):
    queries, keys_all, values_all = (packed[0], packed[1], packed[2])
    scores = jnp.einsum(
        "qhd,khd->hqk", queries, keys_all, preferred_element_type=jnp.float32
    ) * HD ** (-0.5)
    log_total = jax.nn.logsumexp(scores, axis=-1)
    soft_weights = jnp.exp(scores - log_total[..., None]).astype(jnp.bfloat16)
    mixture = jnp.einsum(
        "hqk,khd->qhd", soft_weights, values_all, preferred_element_type=jnp.float32
    ).astype(jnp.bfloat16)
    return (mixture, log_total)


def attend_back(packed):
    triple, mixture, grad_mixture, log_total = packed
    queries, keys_all, values_all = (triple[0], triple[1], triple[2])
    factor = HD ** (-0.5)
    scores = (
        jnp.einsum("qhd,khd->hqk", queries, keys_all, preferred_element_type=jnp.float32) * factor
    )
    soft_exact = jnp.exp(scores - log_total[..., None])
    soft_weights = soft_exact.astype(jnp.bfloat16)
    grad_values = jnp.einsum(
        "hqk,qhd->khd", soft_weights, grad_mixture, preferred_element_type=jnp.float32
    )
    grad_soft = jnp.einsum(
        "qhd,khd->hqk", grad_mixture, values_all, preferred_element_type=jnp.float32
    )
    inner_sum = jnp.sum(grad_mixture.astype(jnp.float32) * mixture.astype(jnp.float32), axis=-1).T
    grad_scores = (soft_exact * (grad_soft - inner_sum[..., None])).astype(jnp.bfloat16)
    grad_queries = (
        jnp.einsum("hqk,khd->qhd", grad_scores, keys_all, preferred_element_type=jnp.float32)
        * factor
    )
    grad_keys = (
        jnp.einsum("hqk,qhd->khd", grad_scores, queries, preferred_element_type=jnp.float32)
        * factor
    )
    return jnp.stack([grad_queries, grad_keys, grad_values])


def body(
    inputs, cond, w_ada, b_ada, w_qkv, b_qv, w_out, b_out, w_fc1, b_fc1, w_fc2, b_fc2, cotangent
):
    local_seqs = cond.shape[0]
    col_width = inputs.shape[1]
    group_rows = inputs.shape[0] * lax.axis_size("row")
    group_seqs = group_rows // LATENT_TOKENS
    head_width = b_qv.shape[1]
    local_heads = head_width // HD
    act_cond = jax.nn.silu(cond).astype(jnp.bfloat16)
    modulation = (
        jnp.einsum("sd,dke->ske", act_cond, w_ada, preferred_element_type=jnp.float32) + b_ada[None]
    )
    shift_one, scale_one, gate_one = (
        modulation[:, 0, None, :],
        modulation[:, 1, None, :],
        modulation[:, 2, None, :],
    )
    shift_two, scale_two, gate_two = (
        modulation[:, 3, None, :],
        modulation[:, 4, None, :],
        modulation[:, 5, None, :],
    )
    residual = inputs.reshape(local_seqs, LATENT_TOKENS, col_width)
    normed_one, inverse_one = norm_stats(residual)
    hidden_one = (
        (normed_one * (1.0 + scale_one) + shift_one).astype(jnp.bfloat16).reshape(-1, col_width)
    )
    hidden_one_all = rows_forward(hidden_one)
    qkv_sum = cols_forward_sum(
        jnp.einsum("td,kde->kte", hidden_one_all, w_qkv, preferred_element_type=jnp.float32)
    )
    qkv_bias = jnp.stack([b_qv[0], jnp.zeros_like(b_qv[0]), b_qv[1]])
    qkv_low = (qkv_sum + qkv_bias[:, None, :]).astype(jnp.bfloat16)
    qkv_seq = jnp.moveaxis(qkv_low.reshape(3, group_seqs, LATENT_TOKENS, local_heads, HD), 1, 0)
    mixture_seq, log_totals = lax.map(attend, qkv_seq)
    mixture = mixture_seq.reshape(group_rows, head_width)
    mixture_all = cols_forward(mixture)
    attn_out = (
        rows_forward_sum(jnp.dot(mixture_all, w_out, preferred_element_type=jnp.float32)) + b_out
    )
    attn_out = attn_out.reshape(local_seqs, LATENT_TOKENS, col_width)
    middle = residual + gate_one * attn_out
    normed_two, inverse_two = norm_stats(middle)
    hidden_two = (
        (normed_two * (1.0 + scale_two) + shift_two).astype(jnp.bfloat16).reshape(-1, col_width)
    )
    hidden_two_all = rows_forward(hidden_two)
    pre_act = (
        cols_forward_sum(jnp.dot(hidden_two_all, w_fc1, preferred_element_type=jnp.float32)[None])[
            0
        ]
        + b_fc1
    )
    activated = gelu_tanh(pre_act).astype(jnp.bfloat16)
    activated_all = cols_forward(activated)
    mlp_out = (
        rows_forward_sum(jnp.dot(activated_all, w_fc2, preferred_element_type=jnp.float32)) + b_fc2
    )
    mlp_out = mlp_out.reshape(local_seqs, LATENT_TOKENS, col_width)
    result = middle + gate_two * mlp_out
    grad_out = cotangent.reshape(local_seqs, LATENT_TOKENS, col_width)
    grad_mlp = grad_out * gate_two
    grad_gate_two = jnp.sum(grad_out * mlp_out, axis=1)
    bias_fc2 = jnp.sum(grad_mlp, axis=(0, 1))
    grad_mlp_all = rows_backward(grad_mlp.astype(jnp.bfloat16).reshape(-1, col_width))
    act_back = cols_forward(activated)
    gradient_second_dense_weight = jnp.einsum(
        "tf,te->fe", act_back, grad_mlp_all, preferred_element_type=jnp.float32
    )
    grad_act = cols_backward_sum(
        jnp.einsum("te,fe->tf", grad_mlp_all, w_fc2, preferred_element_type=jnp.float32)
    )
    grad_pre = jax.vjp(gelu_tanh, pre_act)[1](grad_act)[0]
    bias_fc1 = jnp.sum(grad_pre, axis=0)
    grad_pre_all = cols_backward(grad_pre.astype(jnp.bfloat16)[None])[0]
    hidden_two_back = rows_forward(hidden_two)
    gradient_first_dense_weight = jnp.einsum(
        "td,tf->df", hidden_two_back, grad_pre_all, preferred_element_type=jnp.float32
    )
    gradient_second_hidden = rows_backward_sum(
        jnp.einsum("tf,df->td", grad_pre_all, w_fc1, preferred_element_type=jnp.float32)
    )
    gradient_second_hidden = gradient_second_hidden.reshape(local_seqs, LATENT_TOKENS, col_width)
    grad_shift_two = jnp.sum(gradient_second_hidden, axis=1)
    grad_scale_two = jnp.sum(gradient_second_hidden * normed_two, axis=1)
    grad_middle = grad_out + norm_back(
        gradient_second_hidden * (1.0 + scale_two), normed_two, inverse_two
    )
    grad_attn = grad_middle * gate_one
    grad_gate_one = jnp.sum(grad_middle * attn_out, axis=1)
    bias_out = jnp.sum(grad_attn, axis=(0, 1))
    grad_attn_all = rows_backward(grad_attn.astype(jnp.bfloat16).reshape(-1, col_width))
    mixture_back = cols_forward(mixture)
    gradient_output_weight = jnp.einsum(
        "th,te->he", mixture_back, grad_attn_all, preferred_element_type=jnp.float32
    )
    grad_mixture = cols_backward_sum(
        jnp.einsum("te,he->th", grad_attn_all, w_out, preferred_element_type=jnp.float32)
    )
    grad_mixture_seq = grad_mixture.astype(jnp.bfloat16).reshape(
        group_seqs, LATENT_TOKENS, local_heads, HD
    )
    grad_qkv_seq = lax.map(attend_back, (qkv_seq, mixture_seq, grad_mixture_seq, log_totals))
    grad_qkv = jnp.moveaxis(grad_qkv_seq, 0, 1).reshape(3, group_rows, head_width)
    bias_qv = jnp.stack([jnp.sum(grad_qkv[0], axis=0), jnp.sum(grad_qkv[2], axis=0)])
    grad_qkv_all = cols_backward(grad_qkv.astype(jnp.bfloat16))
    hidden_one_back = rows_forward(hidden_one)
    gradient_query_key_value_weight = jnp.einsum(
        "td,kte->kde", hidden_one_back, grad_qkv_all, preferred_element_type=jnp.float32
    )
    grad_hidden_one = rows_backward_sum(
        jnp.einsum("kte,kde->td", grad_qkv_all, w_qkv, preferred_element_type=jnp.float32)
    )
    grad_hidden_one = grad_hidden_one.reshape(local_seqs, LATENT_TOKENS, col_width)
    grad_shift_one = jnp.sum(grad_hidden_one, axis=1)
    grad_scale_one = jnp.sum(grad_hidden_one * normed_one, axis=1)
    grad_inputs = grad_middle + norm_back(
        grad_hidden_one * (1.0 + scale_one), normed_one, inverse_one
    )
    grad_modulation = jnp.stack(
        [
            grad_shift_one,
            grad_scale_one,
            grad_gate_one,
            grad_shift_two,
            grad_scale_two,
            grad_gate_two,
        ],
        axis=1,
    )
    grad_w_ada = jnp.einsum(
        "sd,ske->dke",
        act_cond.astype(jnp.float32),
        grad_modulation,
        precision=lax.Precision.HIGHEST,
        preferred_element_type=jnp.float32,
    )
    bias_ada = jnp.sum(grad_modulation, axis=0)
    grad_silu = lax.psum(
        jnp.einsum(
            "ske,dke->sd",
            grad_modulation,
            w_ada.astype(jnp.float32),
            precision=lax.Precision.HIGHEST,
            preferred_element_type=jnp.float32,
        ),
        "col",
    )
    grad_cond = jax.vjp(jax.nn.silu, cond)[1](grad_silu)[0]
    sharded = (
        lax.psum(gradient_query_key_value_weight.astype(jnp.bfloat16), "dp").astype(jnp.float32),
        lax.psum(bias_qv.astype(jnp.bfloat16), "dp").astype(jnp.float32),
        lax.psum(gradient_output_weight.astype(jnp.bfloat16), "dp").astype(jnp.float32),
        lax.psum(gradient_first_dense_weight.astype(jnp.bfloat16), "dp").astype(jnp.float32),
        lax.psum(bias_fc1.astype(jnp.bfloat16), "dp").astype(jnp.float32),
        lax.psum(gradient_second_dense_weight.astype(jnp.bfloat16), "dp").astype(jnp.float32),
    )
    shared = (
        lax.psum(grad_w_ada.astype(jnp.bfloat16), ("dp", "row")).astype(jnp.float32),
        lax.psum(bias_ada.astype(jnp.bfloat16), ("dp", "row")).astype(jnp.float32),
        lax.psum(bias_out.astype(jnp.bfloat16), ("dp", "row")).astype(jnp.float32),
        lax.psum(bias_fc2.astype(jnp.bfloat16), ("dp", "row")).astype(jnp.float32),
    )
    return (
        result.reshape(-1, col_width),
        grad_inputs.reshape(-1, col_width),
        grad_cond,
        shared[0],
        shared[1],
        sharded[0],
        sharded[1],
        sharded[2],
        shared[2],
        sharded[3],
        sharded[4],
        sharded[5],
        shared[3],
    )


def solution(mesh):
    return jax.shard_map(
        body,
        mesh=mesh,
        in_specs=(
            P(("dp", "row"), "col"),
            P(("dp", "row"), None),
            P(None, None, "col"),
            P(None, "col"),
            P(None, "col", "row"),
            P(None, ("row", "col")),
            P("row", "col"),
            P("col"),
            P("col", "row"),
            P(("row", "col")),
            P("row", "col"),
            P("col"),
            P(("dp", "row"), "col"),
        ),
        out_specs=(
            P(("dp", "row"), "col"),
            P(("dp", "row"), "col"),
            P(("dp", "row"), None),
            P(None, None, "col"),
            P(None, "col"),
            P(None, "col", "row"),
            P(None, ("row", "col")),
            P("row", "col"),
            P("col"),
            P("col", "row"),
            P(("row", "col")),
            P("row", "col"),
            P("col"),
        ),
        check_vma=False,
    )
```

profile of v0, /device:TPU:0, one launch (start us, length us, event | category | flops | bytes accessed | tf_op | source)
XLA Modules:
  0.0 1239.4 jit_solution(17435969472687260025)
XLA Ops:
  12.1 8.6 all-reduce.3
  23.7 21.7 %all-gather.10.cloned.1.call-done = bf16[2048,256]{1,0:T(8,128)(2,1)} async-done(((bf16[1024,256]{1,0:T(8,128)(2,1)}), bf16[2048,256]{1,0:T(8,128)(2,1)}) %all-gather.10.cloned.1.call-update) | async-done | bytes 1048592 | tf_op jit(solution)/shard_map/all_gather | solution.py:37
  45.4 7.8 convolution_bitcast_fusion.1
  54.0 96.6 %reduce-scatter.9.cloned.1.call-done = f32[3,2048,128]{2,1,0:T(8,128)} async-done(((f32[3,2048,512]{2,1,0:T(8,128)}), f32[3,2048,128]{2,1,0:T(8,128)}) %reduce-scatter.9.cloned.1.call-update) | async-done | bytes 3145744 | tf_op jit(solution)/shard_map/reduce_scatter | solution.py:45
  163.2 22.7 %while.22 = (s32[]{:T(128)}, bf16[2,1024,2,64]{1,3,2,0:T(8,128)(2,1)}, f32[2,2,1024]{2,1,0:T(2,128)S(1)}, bf16[2,3,1024,2,64]{2,4,3,1,0:T(8,128)(2,1)}, s32[]{:T(128)}, /*index=5*/s32[]{:T(128)}, s32[]{}, s32[]{}) while((s32[]{:T(128)}, bf16[2,1024,2,64]{1,3,2,0:T(8,128)(2,1)}, f32[2,2,1024]{2,1,0:T(2,128)S(1)}, ...), condition=%wide.region_8.9_spmd, body=%wide.region_5.8_spmd.sunk | while | flops 553795584 | bytes 59869332 | solution.py:144
  188.5 22.6 %all-gather.12.cloned.1.call-done = bf16[2048,512]{0,1:T(8,128)(2,1)} async-done(((bf16[2048,128]{0,1:T(8,128)(2,1)}), bf16[2048,512]{0,1:T(8,128)(2,1)}) %all-gather.12.cloned.1.call-update) | async-done | bytes 2097168 | tf_op jit(solution)/shard_map/all_gather | solution.py:41
  217.1 29.8 %reduce-scatter.11.cloned.1.call-done = f32[1024,256]{1,0:T(8,128)} async-done(((f32[2048,256]{1,0:T(8,128)}), f32[1024,256]{1,0:T(8,128)}) %reduce-scatter.11.cloned.1.call-update) | async-done | bytes 1048592 | tf_op jit(solution)/shard_map/reduce_scatter | solution.py:49
  258.8 11.4 all-gather.18.cloned.1.call-done
  270.2 10.0 fusion.57
  280.3 13.2 %all-gather.14.cloned.1.call-done = bf16[2048,256]{1,0:T(8,128)(2,1)} async-done(((bf16[1024,256]{1,0:T(8,128)(2,1)}), bf16[2048,256]{1,0:T(8,128)(2,1)}) %all-gather.14.cloned.1.call-update) | async-done | bytes 1048592 | tf_op jit(solution)/shard_map/all_gather | solution.py:37
  293.5 10.8 convolution_bitcast_fusion
  304.4 116.6 %reduce-scatter.17.cloned.1.call-done = f32[2048,512]{1,0:T(8,128)} async-done(((f32[2048,2048]{1,0:T(8,128)}), f32[2048,512]{1,0:T(8,128)}) %reduce-scatter.17.cloned.1.call-update) | async-done | bytes 4194320 | tf_op jit(solution)/shard_map/reduce_scatter | solution.py:61
  421.0 127.5 %reduce-scatter.13.cloned.1.call-done = f32[1,2048,512]{2,1,0:T(8,128)} async-done(((f32[1,2048,2048]{2,1,0:T(8,128)}), f32[1,2048,512]{2,1,0:T(8,128)}) %reduce-scatter.13.cloned.1.call-update) | async-done | bytes 4194320 | tf_op jit(solution)/shard_map/reduce_scatter | solution.py:45
  556.0 57.8 %all-gather.24.cloned.1.call-done = bf16[2048,2048]{1,0:T(8,128)(2,1)} async-done(((bf16[2048,512]{1,0:T(8,128)(2,1)}), bf16[2048,2048]{1,0:T(8,128)(2,1)}) %all-gather.24.cloned.1.call-update) | async-done | bytes 8388624 | tf_op jit(solution)/shard_map/all_gather | solution.py:57
  613.8 7.3 fusion.58
  621.2 52.9 %all-gather.16.cloned.1.call-done = bf16[2048,2048]{1,0:T(8,128)(2,1)} async-done(((bf16[2048,512]{1,0:T(8,128)(2,1)}), bf16[2048,2048]{1,0:T(8,128)(2,1)}) %all-gather.16.cloned.1.call-update) | async-done | bytes 8388624 | tf_op jit(solution)/shard_map/all_gather | solution.py:41
  674.1 7.3 fusion.56
  681.6 27.2 %reduce-scatter.19.cloned.1.call-done = f32[1024,256]{1,0:T(8,128)} async-done(((f32[2048,256]{1,0:T(8,128)}), f32[1024,256]{1,0:T(8,128)}) %reduce-scatter.19.cloned.1.call-update) | async-done | bytes 1048592 | tf_op jit(solution)/shard_map/reduce_scatter | solution.py:65
  717.5 25.9 %reduce-scatter.15.cloned.1.call-done = f32[1024,256]{1,0:T(8,128)} async-done(((f32[2048,256]{1,0:T(8,128)}), f32[1024,256]{1,0:T(8,128)}) %reduce-scatter.15.cloned.1.call-update) | async-done | bytes 1048592 | tf_op jit(solution)/shard_map/reduce_scatter | solution.py:49
  749.1 21.4 %all-gather.20.cloned.1.call-done = bf16[2048,256]{1,0:T(8,128)(2,1)} async-done(((bf16[1024,256]{1,0:T(8,128)(2,1)}), bf16[2048,256]{1,0:T(8,128)(2,1)}) %all-gather.20.cloned.1.call-update) | async-done | bytes 1048592 | tf_op jit(solution)/shard_map/all_gather | solution.py:53
  774.5 44.5 %reduce-scatter.21.cloned.1.call-done = f32[2048,128]{1,0:T(8,128)} async-done(((f32[2048,512]{1,0:T(8,128)}), f32[2048,128]{1,0:T(8,128)}) %reduce-scatter.21.cloned.1.call-update) | async-done | bytes 1048592 | tf_op jit(solution)/shard_map/reduce_scatter | solution.py:61
  827.8 38.4 %while.23 = (s32[]{:T(128)}, f32[2,3,1024,2,64]{2,4,3,1,0:T(8,128)}, bf16[2,3,1024,2,64]{2,4,3,1,0:T(8,128)(2,1)}, f32[2,2,1024]{2,1,0:T(2,128)S(1)}, bf16[2,102...) while((s32[]{:T(128)}, ...), condition=%wide.region_25.26_spmd, body=%wide.region_23.25_spmd.sunk | while | flops 1360525312 | bytes 84725512 | solution.py:212
  869.5 8.4 copy.49
  884.4 47.0 %all-gather.22.cloned.1.call-done = bf16[3,2048,512]{2,1,0:T(8,128)(2,1)} async-done(((bf16[3,2048,128]{2,1,0:T(8,128)(2,1)}), bf16[3,2048,512]{2,1,0:T(8,128)(2,1)}) %all-gather.22.cloned.1.call-update) | async-done | bytes 6291472 | tf_op jit(solution)/shard_map/all_gather | solution.py:57
  937.7 7.2 convolution_convert_fusion.1
  944.9 7.0 convolution_convert_fusion
  956.2 13.4 %reduce-scatter.23.cloned.1.call-done = f32[1024,256]{1,0:T(8,128)} async-done(((f32[2048,256]{1,0:T(8,128)}), f32[1024,256]{1,0:T(8,128)}) %reduce-scatter.23.cloned.1.call-update) | async-done | bytes 1048592 | tf_op jit(solution)/shard_map/reduce_scatter | solution.py:65
  975.9 12.4 all-reduce.5
  989.4 105.0 %all-reduce.12.cloned.1.call-done = (bf16[3,256,512]{1,2,0:T(8,128)(2,1)}, bf16[512,256]{1,0:T(8,128)(2,1)}, bf16[256,2048]{1,0:T(8,128)(2,1)}, bf16[2048,256]{1,0:T(8,128)(2,1)}) async-done(((bf16[3,256,512]{1,2,0:T(8,128)(2,1)}, bf16[512,256]{1,0:T(8,128)(2,1)}, bf16[256,2048]{1,0:T(8,128)(2,1)}, bf16[2048,256]{1,0:T(8,128)(2,1)}), (bf16[3,256,512]{1,2,0:T(8,128)(2,1)}, bf16[512,256]{1,0:T(8,128)(2,1)}, ...) | async-done | bytes 3145744 | tf_op jit(solution)/shard_map/psum | solution.py:260
  1103.4 21.2 %all-reduce.4 = (bf16[6,256]{1,0:T(8,128)(2,1)S(1)}, bf16[256]{0:T(256)(128)(2,1)S(1)}, bf16[256]{0:T(256)(128)(2,1)S(1)}) all-reduce(bf16[6,256]{1,0:T(8,128)(2,1)S(1)} %bitcast_convert_fusion, bf16[256]{0:T(256)(128)(2,1)S(1)} %get-tuple-element.180, ...), channel_id=1, replica_groups=mesh['dp'=4,'row'=2,'col'=4] {'dp','row'}, use_global_device_ids=true, to_apply=%region_39.40 | all-reduce | flops 2048 | bytes 8192 | tf_op jit(solution)/shard_map/psum | solution.py:269
  1128.9 10.9 all-reduce
  1143.5 83.4 %all-reduce.10.cloned.1.call-done = bf16[1024,6,256]{2,0,1:T(8,128)(2,1)} async-done(((bf16[1024,6,256]{2,0,1:T(8,128)(2,1)}), bf16[1024,6,256]{2,0,1:T(8,128)(2,1)}) %all-reduce.10.cloned.1.call-update) | async-done | bytes 3145744 | tf_op jit(solution)/shard_map/psum | solution.py:268
  (198 shorter events, 187.2 us)
Async XLA Ops:
  7.2 38.2 %all-gather.10.cloned.1.call-start = ((), (), s32[]{:S(2)}) async-start(), calls=%async_computation.8 | async-start | bytes 1572864 | tf_op jit(solution)/shard_map/all_gather | solution.py:37
  12.1 41.1 %copy-start.20 = (f32[1,1,256]{2,1,0:T(1,128)}, f32[1,1,256]{2,1,0:T(1,128)S(1)}, u32[]{:S(2)}) copy-start(f32[1,1,256]{2,1,0:T(1,128)S(1)} %get-tuple-element.186) | copy-start | bytes 3076
  23.7 126.9 %reduce-scatter.9.cloned.1.call-start = ((), (), s32[]{:S(2)}) async-start(), calls=%async_computation.9 | async-start | bytes 15728640 | tf_op jit(solution)/shard_map/reduce_scatter | solution.py:45
  53.3 157.9 %all-gather.12.cloned.1.call-start = ((), (), s32[]{:S(2)}) async-start(), calls=%async_computation.10 | async-start | bytes 2621440 | tf_op jit(solution)/shard_map/all_gather | solution.py:41
  163.2 47.9 %copy-start.9 = (bf16[512,256]{1,0:T(8,128)(2,1)S(1)}, bf16[512,256]{1,0:T(8,128)(2,1)}, u32[]{:S(2)}) copy-start(bf16[512,256]{1,0:T(8,128)(2,1)} %param.23) | copy-start | bytes 786436
  188.5 58.5 %copy-start.24 = (f32[256]{0:T(256)S(1)}, f32[256]{0:T(256)}, u32[]{:S(2)}) copy-start(f32[256]{0:T(256)} %param.24) | copy-start | bytes 3076
  188.5 58.5 %reduce-scatter.11.cloned.1.call-start = ((), (), s32[]{:S(2)}) async-start(), calls=%async_computation.11 | async-start | bytes 3145728 | tf_op jit(solution)/shard_map/reduce_scatter | solution.py:49
  214.9 55.3 %all-gather.18.cloned.1.call-start = ((), (), s32[]{:S(2)}) async-start(), calls=%async_computation.16 | async-start | bytes 1572864 | tf_op jit(solution)/shard_map/all_gather | solution.py:53
  217.0 76.5 %all-gather.14.cloned.1.call-start = ((), (), s32[]{:S(2)}) async-start(), calls=%async_computation.12 | async-start | bytes 1572864 | tf_op jit(solution)/shard_map/all_gather | solution.py:37
  258.5 162.5 %reduce-scatter.17.cloned.1.call-start = ((), (), s32[]{:S(2)}) async-start(), calls=%async_computation.17 | async-start | bytes 20971520 | tf_op jit(solution)/shard_map/reduce_scatter | solution.py:61
  280.2 268.3 %reduce-scatter.13.cloned.1.call-start = ((), (), s32[]{:S(2)}) async-start(), calls=%async_computation.13 | async-start | bytes 20971520 | tf_op jit(solution)/shard_map/reduce_scatter | solution.py:45
  304.3 244.2 %copy-start.25 = (f32[512]{0:T(512)S(1)}, f32[512]{0:T(512)}, u32[]{:S(2)}) copy-start(f32[512]{0:T(512)} %param.26) | copy-start | bytes 6148
  304.3 309.4 %all-gather.24.cloned.1.call-start = ((), (), s32[]{:S(2)}) async-start(), calls=%async_computation.24 | async-start | bytes 10485760 | tf_op jit(solution)/shard_map/all_gather | solution.py:57
  555.4 118.7 %all-gather.16.cloned.1.call-start = ((), (), s32[]{:S(2)}) async-start(), calls=%async_computation.14 | async-start | bytes 10485760 | tf_op jit(solution)/shard_map/all_gather | solution.py:41
  556.0 152.9 %reduce-scatter.19.cloned.1.call-start = ((), (), s32[]{:S(2)}) async-start(), calls=%async_computation.18 | async-start | bytes 3145728 | tf_op jit(solution)/shard_map/reduce_scatter | solution.py:65
  621.1 122.3 %reduce-scatter.15.cloned.1.call-start = ((), (), s32[]{:S(2)}) async-start(), calls=%async_computation.15 | async-start | bytes 3145728 | tf_op jit(solution)/shard_map/reduce_scatter | solution.py:49
  681.3 62.1 %copy-start.26 = (f32[256]{0:T(256)S(1)}, f32[256]{0:T(256)}, u32[]{:S(2)}) copy-start(f32[256]{0:T(256)} %param.28) | copy-start | bytes 3076
  681.4 89.1 %all-gather.20.cloned.1.call-start = ((), (), s32[]{:S(2)}) async-start(), calls=%async_computation.19 | async-start | bytes 1572864 | tf_op jit(solution)/shard_map/all_gather | solution.py:53
  749.0 70.0 %reduce-scatter.21.cloned.1.call-start = ((), (), s32[]{:S(2)}) async-start(), calls=%async_computation.20 | async-start | bytes 5242880 | tf_op jit(solution)/shard_map/reduce_scatter | solution.py:61
  774.5 157.0 %all-gather.22.cloned.1.call-start = ((), (), s32[]{:S(2)}) async-start(), calls=%async_computation.21 | async-start | bytes 7864320 | tf_op jit(solution)/shard_map/all_gather | solution.py:57
  884.1 85.5 %reduce-scatter.23.cloned.1.call-start = ((), (), s32[]{:S(2)}) async-start(), calls=%async_computation.22 | async-start | bytes 3145728 | tf_op jit(solution)/shard_map/reduce_scatter | solution.py:65
  937.6 156.9 %all-reduce.12.cloned.1.call-start = ((), (), s32[]{:S(2)}) async-start(), calls=%async_computation.25 | async-start | bytes 6291456 | tf_op jit(solution)/shard_map/psum | solution.py:260
  937.7 15.6 %slice-start = ((s8[6291456]{0:T(1024)(128)(4,1)}), s8[4194304]{0:T(1024)(128)(4,1)S(1)}, s32[]{:S(2)}) async-start(s8[6291456]{0:T(1024)(128)(4,1)} %bitcast.256), calls=%async_computation.26 | async-start | bytes 8388608
  944.8 8.5 copy-start.10
  944.8 8.5 slice-start.1
  953.3 16.3 %copy-start.14 = (f32[1,1024]{1,0:T(1,128)S(1)}, f32[1,1024]{1,0:T(1,128)}, u32[]{:S(2)}) copy-start(f32[1,1024]{1,0:T(1,128)} %copy-done.13) | copy-start | bytes 12292
  953.3 16.3 %copy-start.16 = (f32[1,1024]{1,0:T(1,128)S(1)}, f32[1,1024]{1,0:T(1,128)}, u32[]{:S(2)}) copy-start(f32[1,1024]{1,0:T(1,128)} %copy-done.15) | copy-start | bytes 12292
  953.3 16.3 %copy-start.21 = (f32[1,1,256]{2,1,0:T(1,128)S(1)}, f32[1,1,256]{2,1,0:T(1,128)}, u32[]{:S(2)}) copy-start(f32[1,1,256]{2,1,0:T(1,128)} %copy-done.20) | copy-start | bytes 3076
  956.2 270.8 %all-reduce.10.cloned.1.call-start = ((), (), s32[]{:S(2)}) async-start(), calls=%async_computation.23 | async-start | bytes 6291456 | tf_op jit(solution)/shard_map/psum | solution.py:268
  1094.5 8.1 copy-start.12
  1097.3 42.5 %copy-start.17 = (f32[1,1024]{1,0:T(1,128)S(1)}, f32[1,1024]{1,0:T(1,128)}, u32[]{:S(2)}) copy-start(f32[1,1024]{1,0:T(1,128)} %param.18) | copy-start | bytes 12292
  1097.3 42.5 %copy-start.19 = (f32[1,1024]{1,0:T(1,128)S(1)}, f32[1,1024]{1,0:T(1,128)}, u32[]{:S(2)}) copy-start(f32[1,1024]{1,0:T(1,128)} %copy-done.18) | copy-start | bytes 12292
  (21 other events, 82.9 us)
Sparse Core Ops, SparseCore 0:
  23.8 21.5 all-gather.9
  53.4 97.1 reduce-scatter.8
  188.6 22.5 all-gather.11
  215.0 31.8 reduce-scatter.10
  248.9 21.2 all-gather.17
  272.2 21.2 all-gather.13
  296.1 124.8 reduce-scatter.16
  423.6 124.8 reduce-scatter.12
  555.5 58.2 all-gather.23
  615.8 58.2 all-gather.15
  676.9 31.8 reduce-scatter.18
  711.5 31.8 reduce-scatter.14
  749.1 21.2 all-gather.19
  774.6 44.4 reduce-scatter.20
  884.3 47.1 all-gather.21
  937.7 31.8 reduce-scatter.22
  973.3 121.1 all-reduce.11
  1098.5 128.4 all-reduce.9
where the time goes:
time: 1250 us; the launch traced here: 1240 us
  waiting for transfers between devices  919 us (74%)
  matrix products  131 us (10%)
  blocking collectives  66.1 us (5%)
  other arithmetic  64.8 us (5%)
  local copies, waits for them, and re-layouts  42.5 us (3%)
  between operations  15 us (1%)
    reduce_scatter x2, waiting for transfers between devices, cols_forward_sum(): lax.psum_scatter(partial_value, 'col', scatter_dimension=2, tiled=True)  224 us
    reduce_scatter x2, waiting for transfers between devices, cols_backward_sum(): lax.psum_scatter(partial_value, 'col', scatter_dimension=1, tiled=True)  161 us
    psum x1, waiting for transfers between devices, body(): lax.psum(gradient_query_key_value_weight.astype(jnp.bfloat16), 'dp')  105 us
    all_gather x2, waiting for transfers between devices, cols_backward(): return lax.all_gather(local, 'col', axis=2, tiled=True)  105 us
    psum x1, waiting for transfers between devices, body(): lax.psum(grad_w_ada.astype(jnp.bfloat16), ('dp', 'row')).astype(jnp.float32)  83.4 us
    all_gather x2, waiting for transfers between devices, cols_forward(): return lax.all_gather(local, 'col', axis=1, tiled=True)  75.5 us
    reduce_scatter x2, waiting for transfers between devices, rows_forward_sum(): lax.psum_scatter(partial_value, 'row', scatter_dimension=0, tiled=True)  55.7 us
    reduce_scatter x2, waiting for transfers between devices, rows_backward_sum(): lax.psum_scatter(partial_value, 'row', scatter_dimension=0, tiled=True)  40.6 us
  transfers between devices with their start and end apart: 18, of which 18 were waited for; matrix products, arithmetic and copies ran while one was open for 7% of the time, Pallas kernels for 0%

commit v1 on v0

v1 whole, which is shorter than its diff:
```python
import functools

import jax
import jax.numpy as jnp
from jax import lax
from jax.experimental import pallas as pl
from jax.experimental.pallas import tpu as pltpu
from jax.sharding import PartitionSpec as P

D = 1024
HD = 64
T = 1024
EPSILON = 1e-06
bf16, f32 = jnp.bfloat16, jnp.float32
MESH = pl.DeviceIdType.MESH
NN = ((1,), (0,))
NT = ((1,), (1,))
TN = ((0,), (0,))
FACTOR = HD ** (-0.5)
LOG2E = 1.4426950408889634
GC = 0.7978845608028654
N_SEM = 256


def dot(a, b, dims):
    return lax.dot_general(a, b, (dims, ((), ())), preferred_element_type=f32)


def loop(count, step):
    def one(i, carry):
        step(i)
        return carry

    lax.fori_loop(0, count, one, 0)


def at(start, size):
    if isinstance(start, int):
        return pl.ds(start, size)
    return pl.ds(pl.multiple_of(start, size), size)


def rows_of(i, size):
    return at(i * size, size)


def mega(
    ndp,
    x_hbm,
    cot_hbm,
    wqkv,
    wout,
    wfc1,
    wfc2,
    mod,
    actb,
    bqv,
    bout,
    bfc1,
    bfc2,
    res_o,
    gin_o,
    gq_o,
    go_o,
    g1_o,
    g2_o,
    gm_o,
    act_o,
    gmo_o,
    gbqv_o,
    gbfc1_o,
    gbout_o,
    gbfc2_o,
    gbada_o,
    X,
    COT,
    N1,
    N2,
    ATT,
    WQ,
    WOUT,
    WF1,
    WF2,
    H1,
    MIX,
    H2,
    GM,
    Q,
    K,
    V,
    KT,
    LT,
    L8,
    I8,
    GA,
    DO,
    ACT,
    GPRE,
    SA,
    SAR,
    YA,
    YAR,
    SB,
    SBR,
    YB,
    YBR,
    SC,
    SCR,
    YC,
    YCR,
    ACCA,
    ACCB,
    DQT,
    DK,
    DV,
    QM,
    DOM,
    GQKV,
    X1S,
    X1R,
    ZS1,
    ZR1,
    A1,
    X2S,
    X2R,
    ZS2,
    ZR2,
    A2,
    XQS,
    XQR,
    ZSQ,
    ZRQ,
    AQ,
    XOS,
    XOR,
    ZSO,
    ZRO,
    AO,
    ST,
    CV,
    SBX,
    SVL,
    SVA,
    ACA,
    ss,
    rs,
    ls,
):
    nl = 2 * ndp
    d, r, c = lax.axis_index("dp"), lax.axis_index("row"), lax.axis_index("col")
    me = d * 2 + r
    sib, yc, dg = c + 1 - 2 * (c % 2), (c + 2) % 4, 3 - c
    dev_s, dev_y, dev_g, dev_x = (d, r, sib), (d, r, yc), (d, r, dg), (d, 1 - r, c)
    q_ = 1 - r

    count = [0, 0]

    def sem(k=1):
        base = count[0]
        count[0] += k
        assert count[0] <= ss.shape[0]
        return base

    def lsem(k=1):
        base = count[1]
        count[1] += k
        assert count[1] <= ls.shape[0]
        return base

    def rc(src, dst, i, dev):
        return pltpu.make_async_remote_copy(
            src_ref=src,
            dst_ref=dst,
            send_sem=ss.at[i],
            recv_sem=rs.at[i],
            device_id=dev,
            device_id_type=MESH,
        )

    def lc(src, dst, i):
        return pltpu.make_async_copy(src, dst, ls.at[i])

    finals = []

    lane256 = lax.broadcasted_iota(jnp.int32, (256, 256), 1) // HD
    lane128 = lax.broadcasted_iota(jnp.int32, (128, 128), 1)

    cx, ccot = lc(x_hbm, X, lsem()), lc(cot_hbm, COT, lsem())
    cx.start()
    ccot.start()
    barrier = pltpu.get_barrier_semaphore()
    for dev in (dev_s, dev_y, dev_g):
        pl.semaphore_signal(barrier, inc=1, device_id=dev, device_id_type=MESH)

    def greet(o):
        other = (me + o + 1) % nl
        pl.semaphore_signal(
            barrier, inc=1, device_id=(other // 2, other % 2, c), device_id_type=MESH
        )

    loop(nl - 1, greet)
    pl.semaphore_wait(barrier, nl + 2)

    class Weight:
        def __init__(self, src, dst):
            self.src, self.dst = src, dst
            self.a, self.x, self.l = sem(4), sem(4), lsem()

        def start(self):
            self.local = lc(self.src(c), self.dst(c, r), self.l)
            self.local.start()
            for off in (2, 3, 1):
                to = (c + off) % 4
                cp = rc(self.src(to), self.dst(c, r), self.a + off, (d, r, to))
                cp.start()
                finals.append(cp.wait_send)
            cp = rc(self.src(c), self.dst(c, r), self.x, dev_x)
            cp.start()
            finals.append(cp.wait_send)

        def forward(self, off):
            cs = (c + 4 - off) % 4
            here = self.dst(cs, r)
            rc(here, here, self.a + off, dev_s).wait_recv()
            cp = rc(here, here, self.x + off, dev_x)
            cp.start()
            finals.append(cp.wait_send)

        def wait(self):
            self.local.wait()
            for off in range(4):
                there = self.dst((c + 4 - off) % 4, q_)
                rc(there, there, self.x + off, dev_x).wait_recv()

    w_qkv = Weight(
        lambda c2: wqkv.at[:, :, at(c2 * 128, 128)],
        lambda cs, ro: WQ.at[:, at(cs * 256, 256), at(ro * 128, 128)],
    )
    w_fc1 = Weight(
        lambda c2: wfc1.at[:, at(c2 * 512, 512)],
        lambda cs, ro: WF1.at[at(cs * 256, 256), at(ro * 512, 512)],
    )
    w_fc2 = Weight(
        lambda c2: wfc2.at[at(c2 * 512, 512), :],
        lambda cs, ro: WF2.at[at(ro * 512, 512), at(cs * 256, 256)],
    )
    w_qkv.start()

    SBX[r, 0:1, :] = bfc1[...]
    SBX[r, 1:2, 0:128] = bqv[0:1, :]
    SBX[r, 1:2, 128:256] = bqv[1:2, :]
    sbx = sem()
    cp = rc(SBX.at[r], SBX.at[r], sbx, dev_x)
    cp.start()
    finals.append(cp.wait_send)

    wo, wol = sem(4), lsem(4)
    for cs in range(4):
        place = WOUT.at[at(256 * cs + 128 * r, 128), :]
        cp = rc(wout.at[at(cs * 128, 128), :], place, wo + cs, dev_x)
        cp.start()
        finals.append(cp.wait_send)
        lc(wout.at[at(cs * 128, 128), :], place, wol + cs).start()

    def wait_wout():
        for cs in range(4):
            place = WOUT.at[at(256 * cs + 128 * r, 128), :]
            lc(wout.at[at(cs * 128, 128), :], place, wol + cs).wait()
            there = WOUT.at[at(256 * cs + 128 * q_, 128), :]
            rc(there, there, wo + cs, dev_x).wait_recv()

    class ToAll:
        def __init__(self, buf):
            self.buf, self.s = buf, sem(nl - 1)

        def start(self):
            def one(o):
                other = (me + o + 1) % nl
                rc(self.buf.at[me], self.buf.at[me], self.s + o, (other // 2, other % 2, c)).start()

            loop(nl - 1, one)

        def wait(self):
            def one(o):
                other = (me + nl - o - 1) % nl
                rc(self.buf.at[other], self.buf.at[other], self.s + o, dev_x).wait()

            loop(nl - 1, one)

    class Gather:
        def __init__(self, buf):
            self.buf, self.s = buf, sem(12)
            finals.append(lambda: loop(4, self.drain))

        def reg(self, i, cs):
            return self.buf.at[rows_of(i, 256), at(cs * 256, 256)]

        def start(self, i):
            mine = self.reg(i, c)
            rc(mine, mine, self.s + i, dev_y).start()
            rc(mine, mine, self.s + 4 + i, dev_s).start()

        def forward(self, i):
            theirs = self.reg(i, yc)
            rc(theirs, theirs, self.s + i, dev_y).wait_recv()
            rc(theirs, theirs, self.s + 8 + i, dev_s).start()

        def wait(self, i):
            a, b = self.reg(i, sib), self.reg(i, dg)
            rc(a, a, self.s + 4 + i, dev_s).wait_recv()
            rc(b, b, self.s + 8 + i, dev_s).wait_recv()

        def drain(self, i):
            mine, theirs = self.reg(i, c), self.reg(i, yc)
            rc(mine, mine, self.s + i, dev_y).wait_send()
            rc(mine, mine, self.s + 4 + i, dev_s).wait_send()
            rc(theirs, theirs, self.s + 8 + i, dev_s).wait_send()

    class Scatter:
        def __init__(self, part, snd, srec, ysnd, yrec, acc):
            self.part, self.snd, self.srec = part, snd, srec
            self.ysnd, self.yrec, self.acc = ysnd, yrec, acc
            self.s = sem(8)

        def one(self, i):
            rows = rows_of(i, 256)
            self.snd[rows, 0:256] = self.part(i, dg).astype(bf16)
            self.snd[rows, 256:512] = self.part(i, sib).astype(bf16)
            rc(self.snd.at[rows], self.srec.at[rows], self.s + i, dev_s).start()

        def two(self, i):
            rows = rows_of(i, 256)
            value = self.part(i, yc)
            rc(self.snd.at[rows], self.srec.at[rows], self.s + i, dev_s).wait_recv()
            self.ysnd[rows, :] = (value + self.srec[rows, 0:256].astype(f32)).astype(bf16)
            rc(self.ysnd.at[rows], self.yrec.at[rows], self.s + 4 + i, dev_y).start()

        def three(self, i):
            rows = rows_of(i, 256)
            self.acc[rows, :] = self.part(i, c) + self.srec[rows, 256:512].astype(f32)

        def four(self, i):
            rows = rows_of(i, 256)
            rc(self.ysnd.at[rows], self.yrec.at[rows], self.s + 4 + i, dev_y).wait_recv()
            return self.acc[rows, :] + self.yrec[rows, :].astype(f32)

        def drain(self):
            def one(i):
                rows = rows_of(i, 256)
                rc(self.snd.at[rows], self.srec.at[rows], self.s + i, dev_s).wait_send()
                rc(self.ysnd.at[rows], self.yrec.at[rows], self.s + 4 + i, dev_y).wait_send()

            loop(4, one)

        def launch(self):
            loop(4, self.one)
            loop(4, self.two)
            loop(4, self.three)

    class Stats:
        def __init__(self, e):
            self.e, self.s = e, sem(3)

        def put(self, i, a, b):
            both = jnp.where(lane128 == 0, a, jnp.where(lane128 == 1, b, 0.0)).T
            ST[self.e, c, pl.ds(i, 1), :] = both[0:1, :]
            ST[self.e, c, pl.ds(8 + i, 1), :] = both[1:2, :]

        def exchange(self):
            mine = ST.at[self.e, c]
            for n, dev in enumerate((dev_s, dev_y, dev_g)):
                cp = rc(mine, mine, self.s + n, dev)
                cp.start()
                finals.append(cp.wait_send)

        def total(self):
            for n, (dev, cs) in enumerate(((dev_s, sib), (dev_y, yc), (dev_g, dg))):
                there = ST.at[self.e, cs]
                rc(there, there, self.s + n, dev).wait_recv()
            total = ST[self.e, 0] + ST[self.e, 1] + ST[self.e, 2] + ST[self.e, 3]
            return total[0:8, :], total[8:16, :]

    def column(n, i):
        half = jnp.broadcast_to(CV[n, pl.ds(i, 1), :], (128, 128)).T
        return jnp.concatenate([half, half], axis=1)

    def token_sum(value):
        return jnp.sum(value, axis=0, keepdims=True)

    row_shift1, row_scale1, row_gate1 = mod[0:1, :], 1.0 + mod[1:2, :], mod[2:3, :]
    row_shift2, row_scale2, row_gate2 = mod[3:4, :], 1.0 + mod[4:5, :], mod[5:6, :]
    mine = at(256 * c, 256)
    SVL[...] = jnp.zeros_like(SVL)
    G_SHIFT1, G_SCALE1, G_GATE1 = (2, 0), (2, 256), (3, 0)
    G_SHIFT2, G_SCALE2, G_GATE2 = (3, 256), (4, 0), (4, 256)

    def add_to(where, value):
        row, lane = where
        SVL[row : row + 1, lane : lane + value.shape[1]] += value

    ACA[me] = actb[...]
    aca = ToAll(ACA)
    aca.start()
    st1, st2, st3, st4 = Stats(0), Stats(1), Stats(2), Stats(3)
    cx.wait()

    def n1_sums(i):
        x = X[rows_of(i, 128), :]
        st1.put(i, jnp.sum(x, axis=1, keepdims=True), jnp.sum(x * x, axis=1, keepdims=True))

    loop(8, n1_sums)
    st1.exchange()
    ccot.wait()

    def gm_step(i):
        rows = rows_of(i, 128)
        g = COT[rows, :] * row_gate2
        add_to((6, 256), token_sum(g))
        GM[rows, mine] = g.astype(bf16)

    loop(8, gm_step)
    s1, s2 = st1.total()
    average = s1 / D
    CV[0] = average
    CV[1] = lax.rsqrt(s2 / D - average * average + EPSILON)
    ag_h1, ag_mix, ag_h2, ag_gm = Gather(H1), Gather(MIX), Gather(H2), Gather(GM)

    def n1_norm(i):
        for s in range(2):
            rows = at(i * 256 + s * 128, 128)
            normed = (X[rows, :] - column(0, 2 * i + s)) * column(1, 2 * i + s)
            N1[rows, :] = normed
            H1[rows, mine] = (normed * row_scale1 + row_shift1).astype(bf16)
        ag_h1.start(i)

    loop(4, n1_norm)
    for off in (1, 2, 3):
        w_qkv.forward(off)
    loop(4, ag_h1.forward)
    w_fc1.start()

    there = SBX.at[q_]
    rc(there, there, sbx, dev_x).wait_recv()
    w_qkv.wait()

    def qkv_step(i):
        ag_h1.wait(i)
        rows = rows_of(i, 256)
        h = H1[rows, :]
        qb = jnp.concatenate([SBX[0, 1:2, 0:128], SBX[1, 1:2, 0:128]], axis=1)
        vb = jnp.concatenate([SBX[0, 1:2, 128:256], SBX[1, 1:2, 128:256]], axis=1)
        Q[rows, :] = (dot(h, WQ[0], NN) + qb).astype(bf16)
        K[rows, :] = dot(h, WQ[1], NN).astype(bf16)
        V[rows, :] = (dot(h, WQ[2], NN) + vb).astype(bf16)

    loop(4, qkv_step)

    def att_step(i):
        rows = rows_of(i, 256)
        qt = Q[rows, :]
        out = jnp.zeros((256, 256), f32)
        logs = jnp.zeros((256, 128), f32)
        lane = lax.broadcasted_iota(jnp.int32, (256, 128), 1)
        for h in range(4):
            qm = jnp.where(lane256 == h, qt, jnp.zeros_like(qt))
            s = dot(qm, K[...], NT)
            m = jnp.max(s, axis=1, keepdims=True)
            p = jnp.exp2((s - m) * (FACTOR * LOG2E))
            total = jnp.sum(p, axis=1, keepdims=True)
            o = dot(p.astype(bf16), V[...], NN)
            out = jnp.where(lane256 == h, o / total, out)
            logs = jnp.where(lane == h, m * (FACTOR * LOG2E) + jnp.log2(total), logs)
        MIX[rows, mine] = out.astype(bf16)
        LT[rows, :] = logs
        ag_mix.start(i)

        @pl.when(i >= 2)
        def _():
            ag_mix.forward(i - 2)

    loop(4, att_step)
    for off in (1, 2, 3):
        w_fc1.forward(off)
    ag_mix.forward(2)
    ag_mix.forward(3)
    w_fc2.start()
    loop(4, ag_gm.start)

    wait_wout()

    def out_step(i):
        ag_mix.wait(i)
        rows = rows_of(i, 256)
        att = dot(MIX[rows, :], WOUT[...], NN) + bout[...]
        ATT[rows, :] = att
        X[rows, :] = X[rows, :] + row_gate1 * att

    loop(4, out_step)

    def n2_sums(i):
        x = X[rows_of(i, 128), :]
        st2.put(i, jnp.sum(x, axis=1, keepdims=True), jnp.sum(x * x, axis=1, keepdims=True))

    loop(8, n2_sums)
    st2.exchange()
    s1, s2 = st2.total()
    average = s1 / D
    CV[2] = average
    CV[3] = lax.rsqrt(s2 / D - average * average + EPSILON)

    def n2_norm(i):
        for s in range(2):
            rows = at(i * 256 + s * 128, 128)
            normed = (X[rows, :] - column(2, 2 * i + s)) * column(3, 2 * i + s)
            N2[rows, :] = normed
            H2[rows, mine] = (normed * row_scale2 + row_shift2).astype(bf16)
        ag_h2.start(i)

    loop(4, n2_norm)
    for off in (1, 2, 3):
        w_fc2.forward(off)
    loop(4, ag_gm.forward)
    loop(4, ag_h2.forward)
    w_fc1.wait()
    w_fc2.wait()

    def mlp_step(i):
        ag_gm.wait(i)
        ag_h2.wait(i)
        rows = rows_of(i, 256)
        for j in range(2):
            units = slice(512 * j, 512 * j + 512)
            v = dot(H2[rows, :], WF1[:, units], NN) + SBX[j, 0:1, :]
            g = dot(GM[rows, :], WF2[units, :], NT)
            sq = v * v
            t = jnp.tanh(GC * v * (1.0 + 0.044715 * sq))
            half = 0.5 * (1.0 + t)
            ACT[rows, units] = (v * half).astype(bf16)
            slope = half + (0.5 * GC) * v * (1.0 - t * t) * (1.0 + (3 * 0.044715) * sq)
            g = g * slope
            add_to((j, 0), token_sum(g))
            GPRE[rows, units] = g.astype(bf16)

    loop(4, mlp_step)

    rs_h2 = Scatter(
        lambda i, b: dot(GPRE[rows_of(i, 256), :], WF1[at(b * 256, 256), :], NT),
        SA, SAR, YA, YAR, ACCA,
    )
    rs_h2.launch()

    x1, x2, xq, xo = sem(4), sem(2), sem(4), sem()

    def dw1_step(i):
        h = H2[:, rows_of(i, 256)]
        X1S[i] = dot(h, GPRE[:, at(512 * q_, 512)], TN).astype(bf16)
        rc(X1S.at[i], X1R.at[i], x1 + i, dev_x).start()
        ZS1[i] = dot(h, GPRE[:, at(512 * r, 512)], TN).astype(bf16)

    loop(4, dw1_step)

    rs_out = Scatter(
        lambda i, b: dot(ACT[rows_of(i, 256), :], WF2[:, at(b * 256, 256)], NN),
        SB, SBR, YB, YBR, ACCB,
    )
    rs_out.launch()

    def dw2_step(i):
        rows = rows_of(i, 256)
        X2S[rows, :] = dot(ACT[:, at(512 * q_ + 256 * i, 256)], GM[...], TN).astype(bf16)
        rc(X2S.at[rows], X2R.at[rows], x2 + i, dev_x).start()
        ZS2[rows, :] = dot(ACT[:, at(512 * r + 256 * i, 256)], GM[...], TN).astype(bf16)

    loop(2, dw2_step)

    def b2_sums(i):
        value = rs_h2.four(i)
        ACCA[rows_of(i, 256), :] = value
        for s in range(2):
            rows = at(i * 256 + s * 128, 128)
            gh, normed = ACCA[rows, :], N2[rows, :]
            add_to(G_SHIFT2, token_sum(gh))
            hn = gh * normed
            add_to(G_SCALE2, token_sum(hn))
            st3.put(
                2 * i + s,
                jnp.sum(gh * row_scale2, axis=1, keepdims=True),
                jnp.sum(hn * row_scale2, axis=1, keepdims=True),
            )

    loop(4, b2_sums)
    st3.exchange()
    s1, s2 = st3.total()
    CV[4] = s1 / D
    CV[5] = s2 / D

    def b2_back(i):
        rows = rows_of(i, 128)
        inner = ACCA[rows, :] * row_scale2 - column(4, i) - N2[rows, :] * column(5, i)
        gmid = COT[rows, :] + column(3, i) * inner
        COT[rows, :] = gmid
        ga = gmid * row_gate1
        add_to((6, 0), token_sum(ga))
        add_to(G_GATE1, token_sum(gmid * ATT[rows, :]))
        GA[rows, :] = ga.astype(bf16)

    def out_done(i):
        value = rs_out.four(i) + bfc2[...]
        rows = rows_of(i, 256)
        add_to(G_GATE2, token_sum(COT[rows, :] * value))
        res_o[rows, :] = X[rows, :] + row_gate2 * value

    loop(4, out_done)
    loop(8, b2_back)
    rs_mix = Scatter(
        lambda i, b: dot(GA[rows_of(i, 256), :], WOUT[at(b * 256, 256), :], NT),
        SC, SCR, YC, YCR, ACCA,
    )
    rs_mix.launch()

    def dwo_step(i):
        rows = rows_of(i, 128)
        XOS[rows, :] = dot(MIX[:, at(256 * i + 128 * q_, 128)], GA[...], TN).astype(bf16)
        ZSO[rows, :] = dot(MIX[:, at(256 * i + 128 * r, 128)], GA[...], TN).astype(bf16)

    loop(4, dwo_step)
    rc(XOS, XOR, xo, dev_x).start()

    n1, n2 = 256 // ndp, 512 // ndp
    s_z1, s_z2, s_zq, s_zo = sem(ndp - 1), sem(ndp - 1), sem(ndp - 1), sem(ndp - 1)
    s_a1, s_a2, s_aq = sem(4), sem(4), sem(4)
    l_a1, l_a2, l_aq, l_ao = lsem(), lsem(), lsem(), lsem()
    s_g1, s_g2, s_gq, s_go = sem(ndp - 1), sem(ndp - 1), sem(ndp - 1), sem(ndp - 1)

    def zsend(sets):
        def one(o):
            z = (d + o + 1) % ndp
            for cut, slot, s in sets:
                rc(cut(z), slot(o), s + o, (z, r, c)).start()

        loop(ndp - 1, one)

    def zrecv(sets):
        def one(o):
            z = (d + o + 1) % ndp
            for cut, slot, s in sets:
                rc(cut(z), slot(o), s + o, (z, r, c)).wait()

        loop(ndp - 1, one)

    z1 = (lambda z: ZS1.at[:, at(z * n1, n1), :], lambda o: ZR1.at[o], s_z1)
    z2 = (lambda z: ZS2.at[at(z * n2, n2), :], lambda o: ZR2.at[o], s_z2)
    zq = (lambda z: ZSQ.at[:, :, at(z * n1, n1), :], lambda o: ZRQ.at[o], s_zq)
    zo = (lambda z: ZSO.at[at(z * n2, n2), :], lambda o: ZRO.at[o], s_zo)

    def spread(src, dst, s, l):
        lc(src(c), dst(c), l).start()
        for off in (1, 2, 3):
            to = (c + off) % 4
            cp = rc(src(to), dst(c), s + off, (d, r, to))
            cp.start()
            finals.append(cp.wait_send)

    def spread_wait(src, dst, s, l):
        lc(src(c), dst(c), l).wait()
        for off in (1, 2, 3):
            there = dst((c + 4 - off) % 4)
            rc(there, there, s + off, dev_s).wait_recv()

    sp1 = (lambda c2: A1.at[c2], lambda cs: g1_o.at[at(d * n1, n1), at(512 * cs, 512)], s_a1, l_a1)
    sp2 = (lambda c2: A2.at[:, at(256 * c2, 256)], lambda cs: g2_o.at[cs, at(d * n2, n2), :], s_a2, l_a2)
    spq = (
        lambda c2: AQ.at[c2],
        lambda cs: gq_o.at[:, at(d * n1, n1), at(128 * cs, 128)],
        s_aq,
        l_aq,
    )

    def zspread(sets):
        def one(o):
            z = (d + o + 1) % ndp
            for cut, s in sets:
                rc(cut(d), cut(d), s + o, (z, r, c)).start()

        loop(ndp - 1, one)

        def done(o):
            z = (d + ndp - o - 1) % ndp
            for cut, s in sets:
                rc(cut(z), cut(z), s + o, (z, r, c)).wait()

        finals.append(lambda: loop(ndp - 1, done))

    ag1 = (lambda z: g1_o.at[at(z * n1, n1), :], s_g1)
    ag2 = (lambda z: g2_o.at[:, at(z * n2, n2), :], s_g2)
    agq = (lambda z: gq_o.at[:, at(z * n1, n1), :], s_gq)
    ago = (lambda z: go_o.at[at(z * n2, n2), :], s_go)

    def x1_step(i):
        rc(X1S.at[i], X1R.at[i], x1 + i, dev_x).wait()
        ZS1[i] = (ZS1[i].astype(f32) + X1R[i].astype(f32)).astype(bf16)

    def x2_step(i):
        rows = rows_of(i, 256)
        rc(X2S.at[rows], X2R.at[rows], x2 + i, dev_x).wait()
        ZS2[rows, :] = (ZS2[rows, :].astype(f32) + X2R[rows, :].astype(f32)).astype(bf16)

    loop(4, x1_step)
    zsend([z1])
    loop(2, x2_step)
    zsend([z2])

    def do_step(i):
        DO[rows_of(i, 256), :] = rs_mix.four(i).astype(bf16)

    loop(4, do_step)

    def inner_step(i):
        rows = rows_of(i, 128)
        prod = DO[rows, :].astype(f32) * MIX[rows, mine].astype(f32)
        lane = lax.broadcasted_iota(jnp.int32, (128, 256), 1) // HD
        inner = jnp.zeros((128, 128), f32)
        for h in range(4):
            one = jnp.sum(jnp.where(lane == h, prod, 0.0), axis=1, keepdims=True)
            inner = jnp.where(lane128 == h, one, inner)
        I8[:, rows] = inner.T[0:8, :]
        L8[:, rows] = LT[rows, :].T[0:8, :]

    loop(8, inner_step)

    def kt_step(i):
        rows = rows_of(i, 256)
        KT[:, rows] = K[rows, :].astype(f32).T.astype(bf16)

    loop(4, kt_step)
    DQT[...] = jnp.zeros_like(DQT)
    lane_all = lax.broadcasted_iota(jnp.int32, (1024, 256), 1) // HD

    def head_back(h):
        QM[...] = jnp.where(lane_all == h, Q[...], jnp.zeros_like(Q[...]))
        DOM[...] = jnp.where(lane_all == h, DO[...], jnp.zeros_like(DO[...]))
        lrow, irow = L8[h : h + 1, :], I8[h : h + 1, :]

        def step(i):
            rows = rows_of(i, 512)
            p = jnp.exp2(dot(K[rows, :], QM[...], NT) * (FACTOR * LOG2E) - lrow)
            dp = dot(V[rows, :], DOM[...], NT)
            ds = (p * (dp - irow)).astype(bf16)
            gv, gk = dot(p.astype(bf16), DOM[...], NN), dot(ds, QM[...], NN)
            if h == 0:
                DV[rows, :] = gv
                DK[rows, :] = gk
            else:
                DV[rows, :] += gv
                DK[rows, :] += gk
            DQT[h * HD : (h + 1) * HD, :] += dot(KT[h * HD : (h + 1) * HD, rows], ds, NN)

        loop(2, step)

    head_back(0)
    head_back(1)
    zrecv([z1])
    total = ZS1[:, at(d * n1, n1), :].astype(f32)
    for o in range(ndp - 1):
        total = total + ZR1[o].astype(f32)
    A1[...] = total.astype(bf16)
    spread(*sp1)
    head_back(2)
    spread_wait(*sp1)
    zspread([ag1])
    head_back(3)
    zrecv([z2])
    total = ZS2[at(d * n2, n2), :].astype(f32)
    for o in range(ndp - 1):
        total = total + ZR2[o].astype(f32)
    A2[...] = total.astype(bf16)
    spread(*sp2)

    def gqkv_step(i):
        rows = rows_of(i, 256)
        gq = DQT[:, rows].T * FACTOR
        gk, gv = DK[rows, :] * FACTOR, DV[rows, :]
        add_to((5, 0), token_sum(gq))
        add_to((5, 256), token_sum(gv))
        GQKV[0, rows, :] = gq.astype(bf16)
        GQKV[1, rows, :] = gk.astype(bf16)
        GQKV[2, rows, :] = gv.astype(bf16)

    loop(4, gqkv_step)

    def part_h1(i, b):
        rows, feats = rows_of(i, 256), at(b * 256, 256)
        total = dot(GQKV[0, rows, :], WQ[0, feats, :], NT)
        total = total + dot(GQKV[1, rows, :], WQ[1, feats, :], NT)
        return total + dot(GQKV[2, rows, :], WQ[2, feats, :], NT)

    rs_h2.drain()
    rs_h1 = Scatter(part_h1, SA, SAR, YA, YAR, ACCB)
    loop(4, rs_h1.one)
    loop(4, rs_h1.two)

    def dwq_step(i):
        h = H1[:, rows_of(i, 256)]
        for j in range(3):
            t = dot(h, GQKV[j], TN)
            low, high = t[:, 0:128], t[:, 128:256]
            XQS[i, j] = jnp.where(r == 0, high, low).astype(bf16)
            ZSQ[i, j] = jnp.where(r == 0, low, high).astype(bf16)
        rc(XQS.at[i], XQR.at[i], xq + i, dev_x).start()

    loop(4, dwq_step)
    loop(4, rs_h1.three)
    spread_wait(*sp2)
    zspread([ag2])
    rc(XOS, XOR, xo, dev_x).wait()
    ZSO[...] = (ZSO[...].astype(f32) + XOR[...].astype(f32)).astype(bf16)
    zsend([zo])

    def b1_sums(i):
        value = rs_h1.four(i)
        ACCB[rows_of(i, 256), :] = value
        for s in range(2):
            rows = at(i * 256 + s * 128, 128)
            gh, normed = ACCB[rows, :], N1[rows, :]
            add_to(G_SHIFT1, token_sum(gh))
            hn = gh * normed
            add_to(G_SCALE1, token_sum(hn))
            st4.put(
                2 * i + s,
                jnp.sum(gh * row_scale1, axis=1, keepdims=True),
                jnp.sum(hn * row_scale1, axis=1, keepdims=True),
            )

    loop(4, b1_sums)
    st4.exchange()
    SVA[me] = SVL[...]
    sva = ToAll(SVA)
    sva.start()

    def xq_step(i):
        rc(XQS.at[i], XQR.at[i], xq + i, dev_x).wait()
        ZSQ[i] = (ZSQ[i].astype(f32) + XQR[i].astype(f32)).astype(bf16)

    loop(4, xq_step)
    zsend([zq])
    s1, s2 = st4.total()
    CV[6] = s1 / D
    CV[7] = s2 / D

    def b1_back(i):
        rows = rows_of(i, 128)
        inner = ACCB[rows, :] * row_scale1 - column(6, i) - N1[rows, :] * column(7, i)
        gin_o[rows, :] = COT[rows, :] + column(1, i) * inner

    loop(8, b1_back)

    zrecv([zo])
    total = ZSO[at(d * n2, n2), :].astype(f32)
    for o in range(ndp - 1):
        total = total + ZRO[o].astype(f32)
    AO[...] = total.astype(bf16)
    lc(AO, go_o.at[at(d * n2, n2), :], l_ao).start()
    zrecv([zq])
    total = ZSQ[:, :, at(d * n1, n1), :].astype(f32)
    for o in range(ndp - 1):
        total = total + ZRQ[o].astype(f32)
    AQ[...] = total.astype(bf16)
    spread(*spq)
    lc(AO, go_o.at[at(d * n2, n2), :], l_ao).wait()
    zspread([ago])
    spread_wait(*spq)
    zspread([agq])

    aca.wait()
    sva.wait()
    total = jnp.zeros((8, 512), f32)
    for l in range(nl):
        one = SVA[l]
        total = total + one
        act_o[l : l + 1, :] = ACA[l, 0:1, :]
        for k in range(6):
            gm_o[l, k : k + 1, :] = one[2 + k // 2 : 3 + k // 2, 256 * (k % 2) : 256 * (k % 2) + 256]
        gm_o[l, 6:8, :] = jnp.zeros((2, 256), f32)
    gmo_o[...] = gm_o[me]
    first = r == 0
    for k in range(6):
        gbada_o[k : k + 1, :] = total[2 + k // 2 : 3 + k // 2, 256 * (k % 2) : 256 * (k % 2) + 256]
    gbfc1_o[...] = jnp.where(first, total[0:1, :], total[1:2, :])
    gbqv_o[0:1, :] = jnp.where(first, total[5:6, 0:128], total[5:6, 128:256])
    gbqv_o[1:2, :] = jnp.where(first, total[5:6, 256:384], total[5:6, 384:512])
    gbout_o[...] = total[6:7, 0:256]
    gbfc2_o[...] = total[6:7, 256:512]

    rs_out.drain()
    rs_mix.drain()
    rs_h1.drain()
    for one in finals:
        one()


def call_mega(ndp, *args):
    nl = 2 * ndp
    n1, n2 = 256 // ndp, 512 // ndp
    s = jax.ShapeDtypeStruct
    vmem = pl.BlockSpec(memory_space=pltpu.VMEM)
    hbm = pl.BlockSpec(memory_space=pl.ANY)
    outs = (
        (s((T, 256), f32), vmem),
        (s((T, 256), f32), vmem),
        (s((3, 256, 512), bf16), hbm),
        (s((512, 256), bf16), hbm),
        (s((256, 2048), bf16), hbm),
        (s((4, 512, 256), bf16), hbm),
        (s((nl, 8, 256), f32), vmem),
        (s((nl, D), f32), vmem),
        (s((8, 256), f32), vmem),
        (s((2, 128), f32), vmem),
        (s((1, 512), f32), vmem),
        (s((1, 256), f32), vmem),
        (s((1, 256), f32), vmem),
        (s((6, 256), f32), vmem),
    )

    def v(*shape, t=bf16):
        return pltpu.VMEM(shape, t)

    scratch = (
        [v(T, 256, t=f32)] * 5
        + [v(3, D, 256), v(D, 256), v(D, D), v(D, D)]
        + [v(T, D)] * 4
        + [v(T, 256)] * 3
        + [v(256, T), v(T, 128, t=f32), v(8, T, t=f32), v(8, T, t=f32)]
        + [v(T, 256)] * 2
        + [v(T, D)] * 2
        + [v(T, 512), v(T, 512), v(T, 256), v(T, 256)] * 3
        + [v(T, 256, t=f32)] * 2
        + [v(256, T, t=f32), v(T, 256, t=f32), v(T, 256, t=f32), v(T, 256), v(T, 256), v(3, T, 256)]
        + [v(4, 256, 512)] * 3
        + [v(ndp - 1, 4, n1, 512), v(4, n1, 512)]
        + [v(512, D)] * 3
        + [v(ndp - 1, n2, D), v(n2, D)]
        + [v(4, 3, 256, 128)] * 3
        + [v(ndp - 1, 4, 3, n1, 128), v(4, 3, n1, 128)]
        + [v(512, 256)] * 3
        + [v(ndp - 1, n2, 256), v(n2, 256)]
        + [v(4, 4, 16, 128, t=f32), v(8, 8, 128, t=f32), v(2, 8, 512, t=f32), v(8, 512, t=f32)]
        + [v(nl, 8, 512, t=f32), v(nl, 8, D, t=f32)]
        + [pltpu.SemaphoreType.DMA((N_SEM + 12 * ndp,))] * 2
        + [pltpu.SemaphoreType.DMA((32,))]
    )
    return pl.pallas_call(
        functools.partial(mega, ndp),
        out_shape=[o[0] for o in outs],
        in_specs=[hbm] * 6 + [vmem] * 6,
        out_specs=[o[1] for o in outs],
        scratch_shapes=scratch,
        name="block",
        compiler_params=pltpu.CompilerParams(
            collective_id=0, has_side_effects=True, vmem_limit_bytes=67043328
        ),
    )(*args)


def body(
    inputs, cond, w_ada, b_ada, w_qkv, b_qv, w_out, b_out, w_fc1, b_fc1, w_fc2, b_fc2, cotangent
):
    assert cond.shape[0] == 1 and inputs.shape == (T, 256)
    ndp = lax.axis_size("dp")
    act_cond = jax.nn.silu(cond).astype(bf16)
    modulation = (
        jnp.einsum("sd,dke->ske", act_cond, w_ada, preferred_element_type=f32) + b_ada[None]
    )[0]
    mod8 = jnp.concatenate([modulation, jnp.zeros((2, 256), f32)], axis=0)
    actb = jnp.broadcast_to(act_cond.astype(f32), (8, D))
    (
        result, grad_inputs, gq, go, g1, g2, gm, act_all, gmo, gbqv, gbfc1, gbout, gbfc2, gbada,
    ) = call_mega(
        ndp, inputs, cotangent, w_qkv, w_out, w_fc1, w_fc2, mod8, actb,
        b_qv, b_out[None], b_fc1[None], b_fc2[None],
    )
    grad_w_ada = jnp.einsum(
        "ld,lke->dke", act_all, gm[:, :6], precision=lax.Precision.HIGHEST,
        preferred_element_type=f32,
    )
    grad_silu = lax.psum(
        jnp.einsum(
            "ke,dke->d", gmo[:6], w_ada.astype(f32), precision=lax.Precision.HIGHEST,
            preferred_element_type=f32,
        )[None],
        "col",
    )
    grad_cond = jax.vjp(jax.nn.silu, cond)[1](grad_silu)[0]
    return (
        result,
        grad_inputs,
        grad_cond,
        grad_w_ada,
        gbada,
        gq.astype(f32),
        gbqv,
        go.astype(f32),
        gbout[0],
        g1.astype(f32),
        gbfc1[0],
        g2.reshape(2048, 256).astype(f32),
        gbfc2[0],
    )


def solution(mesh):
    return jax.shard_map(
        body,
        mesh=mesh,
        in_specs=(
            P(("dp", "row"), "col"),
            P(("dp", "row"), None),
            P(None, None, "col"),
            P(None, "col"),
            P(None, "col", "row"),
            P(None, ("row", "col")),
            P("row", "col"),
            P("col"),
            P("col", "row"),
            P(("row", "col")),
            P("row", "col"),
            P("col"),
            P(("dp", "row"), "col"),
        ),
        out_specs=(
            P(("dp", "row"), "col"),
            P(("dp", "row"), "col"),
            P(("dp", "row"), None),
            P(None, None, "col"),
            P(None, "col"),
            P(None, "col", "row"),
            P(None, ("row", "col")),
            P("row", "col"),
            P("col"),
            P("col", "row"),
            P(("row", "col")),
            P("row", "col"),
            P("col"),
        ),
        check_vma=False,
    )
```

time: 1250 us -> 320 us (0.26)
  waiting for transfers between devices: 919 us -> 0 us
  Pallas kernels: 0 us -> 283 us
  matrix products: 131 us -> 13.9 us
  blocking collectives: 66.1 us -> 5.75 us
  other arithmetic: 64.8 us -> 6.63 us
  local copies, waits for them, and re-layouts: 42.5 us -> 7.48 us
  between operations: 15 us -> 0.75 us
    reduce_scatter x8 -> x0, waiting for transfers between devices: 482 us -> none  [the longest x2 224 us: cols_forward_sum(): lax.psum_scatter(partial_value, 'col', scatter_dimension=2, tiled=True)]
    pallas_call x0 -> x1, Pallas kernels: none -> 283 us  [call_mega(): pl.pallas_call(functools.partial(mega, ndp), out_shape=[o[0] for o in out...]
    all_gather x8 -> x0, waiting for transfers between devices: 248 us -> none  [the longest x2 105 us: cols_backward(): return lax.all_gather(local, 'col', axis=2, tiled=True)]
    psum x2 -> x0, waiting for transfers between devices: 188 us -> none  [the longest x1 105 us: body(): lax.psum(gradient_query_key_value_weight.astype(jnp.bfloat16), 'dp')]
    dot_general x28 -> x3, matrix products: 131 us -> 13.9 us  [the longest x1 7.02 us: body(): jnp.einsum('ld,lke->dke', act_all, gm[:, :6], precision=lax.Precision.HIG...]
    psum x6 -> x1, blocking collectives: 66.1 us -> 5.75 us  [body(): lax.psum(jnp.einsum('ke,dke->d', gmo[:6], w_ada.astype(f32), precision=la...]
    convert_element_type x19 -> x5, other arithmetic: 34.2 us -> 6.02 us  [the longest x1 1.56 us: body(): g1.astype(f32)]
    reduce_sum x11 -> x0, other arithmetic: 24 us -> none  [the longest x1 6.84 us: body(): bias_fc1 = jnp.sum(grad_pre, axis=0)]
  transfers between devices with their start and end apart: 18 -> 0, of which waited for: 18 -> 0; matrix products, arithmetic and copies ran while one was open for 7% -> 0% of each run, Pallas kernels for 0% -> 0%
where the time goes in v1:
time: 320 us; the launch traced here: 318 us
  Pallas kernels  283 us (88%)
  matrix products  13.9 us (4%)
  local copies, waits for them, and re-layouts  7.48 us (2%)
  other arithmetic  6.63 us (2%)
  blocking collectives  5.75 us (2%)
    pallas_call x1, Pallas kernels, call_mega(): pl.pallas_call(functools.partial(mega, ndp), out_shape=[o[0] for o in out...  283 us
    dot_general x1, matrix products, body(): jnp.einsum('ld,lke->dke', act_all, gm[:, :6], precision=lax.Precision.HIG...  7.02 us

profile of v1, /device:TPU:0, one launch (start us, length us, event | category | flops | bytes accessed | tf_op | source)
XLA Modules:
  0.0 317.5 jit_solution(2517773326224305432)
XLA Ops:
  0.7 0.7 convert_reduce_fusion
  1.4 0.0 copy-start.8
  1.4 0.6 copy-done.8
  2.0 2.4 fusion.6
  4.4 0.6 concatenate.3.mod
  5.0 0.6 broadcast_in_dim.23.actb
  5.6 283.0 %block.1 = (f32[1024,256]{1,0:T(8,128)}, f32[1024,256]{1,0:T(8,128)}, bf16[3,256,512]{2,1,0:T(8,128)(2,1)}, bf16[512,256]{1,0:T(8,128)(2,1)}, bf16[256,2048]{1,0...) custom-call(f32[1024,256]{1,0:T(8,128)} %x_hbm.1, ...), custom_call_target="tpu_custom_call" | custom-call | tf_op jit(solution)/shard_map/block/pallas_call | solution.py:951
  288.6 0.0 copy-start.7
  288.7 0.0 copy-start.9
  288.7 0.8 slice_bitcast_fusion
  289.5 4.5 %convolution_bitcast_fusion = f32[1,1024]{1,0:T(1,128)S(1)} fusion(bf16[1024,6,256]{2,0,1:T(8,128)(2,1)} %param.15, f32[6,256,1]{1,0,2:T(8,128)S(1)} %slice_bitcast_fusion), kind=kOutput, calls=%fused_computation | convolution fusion | flops 18874368 | bytes 3155968 | tf_op jit(solution)/shard_map/ke,dke->d/dot_general | solution.py:986
  294.0 5.7 %psum.7 = f32[1,1024]{1,0:T(1,128)S(1)} all-reduce(f32[1,1024]{1,0:T(1,128)S(1)} %convolution_bitcast_fusion), channel_id=1, replica_groups=mesh['dp'=4,'row'=2,'col'=4] {'col'}, use_global_device_ids=true, to_apply=%region_0.1 | all-reduce | flops 1024 | bytes 8192 | tf_op jit(solution)/shard_map/psum | solution.py:985
  299.7 0.0 copy-done.7
  299.7 0.6 fusion.5
  300.3 0.8 convert_element_type.22
  301.2 1.4 convert_element_type.21
  302.5 0.0 copy-done.1
  302.5 1.6 convert_element_type.23
  304.1 0.0 copy-done
  304.1 1.5 bitcast_convert_fusion
  305.7 7.0 %fusion = f32[1024,6,256]{2,0,1:T(8,128)} fusion(f32[8,6,256]{2,1,0:T(8,128)S(1)} %bitcast.26, f32[8,1024]{1,0:T(8,128)S(1)} %copy-done.10), kind=kOutput, calls=%fused_computation.2 | convolution fusion | flops 150994944 | bytes 6373376 | tf_op jit(solution)/shard_map/ld,lke->dke/dot_general | solution.py:981
  312.7 0.0 copy-start.13
  312.7 0.0 copy-start.14
  312.7 1.0 copy.41
  313.7 0.0 copy-done.2
  313.7 1.0 copy.42
  314.7 0.6 copy.43
  315.3 0.6 copy.44
  315.8 0.0 copy-done.15
  315.8 0.6 copy.45
  316.4 0.6 copy.46
  317.0 0.6 copy.47
  (24 shorter events, 0.0 us)
Async XLA Ops:
  0.6 3.8 %copy-start.12 = (f32[6,256]{1,0:T(8,128)S(1)}, f32[6,256]{1,0:T(8,128)}, u32[]{:S(2)}) copy-start(f32[6,256]{1,0:T(8,128)} %param.16) | copy-start | bytes 18436
  1.4 0.6 copy-start.8
  288.6 11.1 %copy-start.7 = (f32[1,1024]{1,0:T(1,128)S(1)}, f32[1,1024]{1,0:T(1,128)}, u32[]{:S(2)}) copy-start(f32[1,1024]{1,0:T(1,128)} %param.14) | copy-start | bytes 12292
  288.7 11.1 %copy-start.9 = (f32[1,1024]{1,0:T(1,128)S(1)}, f32[1,1024]{1,0:T(1,128)}, u32[]{:S(2)}) copy-start(f32[1,1024]{1,0:T(1,128)} %copy-done.8) | copy-start | bytes 12292
  288.7 11.7 %copy-start.5 = (bf16[512,256]{1,0:T(8,128)(2,1)S(1)}, bf16[512,256]{1,0:T(8,128)(2,1)}, u32[]{:S(2)}) copy-start(bf16[512,256]{1,0:T(8,128)(2,1)} %get-tuple-element.35) | copy-start | bytes 786436
  288.7 12.5 %copy-start.4 = (bf16[3,256,512]{2,1,0:T(8,128)(2,1)S(1)}, bf16[3,256,512]{2,1,0:T(8,128)(2,1)}, u32[]{:S(2)}) copy-start(bf16[3,256,512]{2,1,0:T(8,128)(2,1)} %get-tuple-element.33) | copy-start | bytes 2359300
  289.5 13.1 %copy-start.1 = (bf16[256,2048]{1,0:T(8,128)(2,1)S(1)}, bf16[256,2048]{1,0:T(8,128)(2,1)}, u32[]{:S(2)}) copy-start(bf16[256,2048]{1,0:T(8,128)(2,1)} %get-tuple-element.37) | copy-start | bytes 3145732
  300.3 3.8 %copy-start = (bf16[4,512,256]{2,1,0:T(8,128)(2,1)S(1)}, bf16[4,512,256]{2,1,0:T(8,128)(2,1)}, u32[]{:S(2)}) copy-start(bf16[4,512,256]{2,1,0:T(8,128)(2,1)} %get-tuple-element.39) | copy-start | bytes 3145732
  302.5 3.1 copy-start.6
  302.5 3.1 copy-start.10
  305.7 7.0 %copy-start.3 = (f32[1024,256]{1,0:T(8,128)S(1)}, f32[1024,256]{1,0:T(8,128)}, u32[]{:S(2)}) copy-start(f32[1024,256]{1,0:T(8,128)} %get-tuple-element.56) | copy-start | bytes 3145732
  305.7 8.0 %copy-start.2 = (f32[1024,256]{1,0:T(8,128)S(1)}, f32[1024,256]{1,0:T(8,128)}, u32[]{:S(2)}) copy-start(f32[1024,256]{1,0:T(8,128)} %get-tuple-element.57) | copy-start | bytes 3145732
  312.7 2.0 copy-start.11
  312.7 2.6 copy-start.16
  312.7 3.1 copy-start.15
  312.7 3.7 %copy-start.13 = (f32[1,512]{1,0:T(1,128)S(1)}, f32[1,512]{1,0:T(1,128)}, u32[]{:S(2)}) copy-start(f32[1,512]{1,0:T(1,128)} %get-tuple-element.38) | copy-start | bytes 6148
  312.7 4.3 %copy-start.14 = (f32[1,256]{1,0:T(1,128)S(1)}, f32[1,256]{1,0:T(1,128)}, u32[]{:S(2)}) copy-start(f32[1,256]{1,0:T(1,128)} %get-tuple-element.40) | copy-start | bytes 3076

commit v2 on v1

v2 whole, which is shorter than its diff:
```python
import functools

import jax
import jax.numpy as jnp
from jax import lax
from jax.experimental import pallas as pl
from jax.experimental.pallas import tpu as pltpu
from jax.sharding import PartitionSpec as P

D = 1024
HD = 64
T = 1024
EPSILON = 1e-06
bf16, f32 = jnp.bfloat16, jnp.float32
MESH = pl.DeviceIdType.MESH
NN = ((1,), (0,))
NT = ((1,), (1,))
TN = ((0,), (0,))
FACTOR = HD ** (-0.5)
LOG2E = 1.4426950408889634
TRACE = False
PLAN = (
    (97, 105, 117.5, 122.5),
    (100, 110, 121, 125.5),
    (107.5, 117.5, 125.5, 131.5),
    (112.5, 121, 131.5, 136),
    (117.5, 128.5, 138, 149),
    (122.5, 131.5, 139.5, 150),
    (128.5, 138, 147, 152),
    (136, 144, 153, 156),
    (138, 147, 155, 156),
    (142.5, 151, 159, 162),
    (147, 156, 164, 167),
    (151, 160, 168, 171),
)
GC = 0.7978845608028654
N_SEM = 256


def dot(a, b, dims):
    return lax.dot_general(a, b, (dims, ((), ())), preferred_element_type=f32)


def loop(count, step):
    def one(i, carry):
        step(i)
        return carry

    lax.fori_loop(0, count, one, 0)


def at(start, size):
    if isinstance(start, int):
        return pl.ds(start, size)
    return pl.ds(pl.multiple_of(start, size), size)


def rows_of(i, size):
    return at(i * size, size)


def mega(
    ndp,
    x_hbm,
    cot_hbm,
    wqkv,
    wout,
    wfc1,
    wfc2,
    mod,
    actb,
    bqv,
    bout,
    bfc1,
    bfc2,
    res_o,
    gin_o,
    gq_o,
    go_o,
    g1_o,
    g2_o,
    gm_o,
    act_o,
    gmo_o,
    gbqv_o,
    gbfc1_o,
    gbout_o,
    gbfc2_o,
    gbada_o,
    X,
    COT,
    N1,
    N2,
    ATT,
    WQ,
    WOUT,
    WF1,
    WF2,
    H1,
    MIX,
    H2,
    GM,
    Q,
    K,
    V,
    KT,
    LT,
    L8,
    I8,
    GA,
    ACT,
    GPRE,
    SA,
    SAR,
    YA,
    YAR,
    SC,
    SCR,
    YC,
    YCR,
    ACCA,
    DQT,
    DK,
    DV,
    QM,
    DOM,
    GQKV,
    X1S,
    X1R,
    ZS1,
    ZR1,
    ZC1,
    X2S,
    X2R,
    ZS2,
    ZR2,
    ZC2,
    XQS,
    XQR,
    ZSQ,
    ZRQ,
    ZCQ,
    XOS,
    XOR,
    ZSO,
    ZRO,
    ZCO,
    ST,
    CV,
    SBX,
    SVL,
    SVA,
    ACA,
    BQV,
    ss,
    rs,
    ls,
):
    nl = 2 * ndp
    DO = GA
    d, r, c = lax.axis_index("dp"), lax.axis_index("row"), lax.axis_index("col")
    me = d * 2 + r
    sib, yc, dg = c + 1 - 2 * (c % 2), (c + 2) % 4, 3 - c
    dev_s, dev_y, dev_g, dev_x = (d, r, sib), (d, r, yc), (d, r, dg), (d, 1 - r, c)
    q_ = 1 - r

    count = [0, 0]

    def sem(k=1):
        base = count[0]
        count[0] += k
        assert count[0] <= ss.shape[0]
        return base

    def lsem(k=1):
        base = count[1]
        count[1] += k
        assert count[1] <= ls.shape[0]
        return base

    def rc(src, dst, i, dev):
        return pltpu.make_async_remote_copy(
            src_ref=src,
            dst_ref=dst,
            send_sem=ss.at[i],
            recv_sem=rs.at[i],
            device_id=dev,
            device_id_type=MESH,
        )

    def lc(src, dst, i):
        return pltpu.make_async_copy(src, dst, ls.at[i])

    finals = []
    scope = []

    def phase(name):
        if TRACE:
            if scope:
                scope.pop().__exit__(None, None, None)
            if name:
                scope.append(jax.named_scope(name))
                scope[-1].__enter__()

    lane256 = lax.broadcasted_iota(jnp.int32, (256, 256), 1) // HD
    lane128 = lax.broadcasted_iota(jnp.int32, (128, 128), 1)

    phase("p00_start")
    cx, ccot = lc(x_hbm, X, lsem()), lc(cot_hbm, COT, lsem())
    cx.start()
    ccot.start()
    barrier = pltpu.get_barrier_semaphore()
    for dev in (dev_s, dev_y, dev_g):
        pl.semaphore_signal(barrier, inc=1, device_id=dev, device_id_type=MESH)

    def greet(o):
        other = (me + o + 1) % nl
        pl.semaphore_signal(
            barrier, inc=1, device_id=(other // 2, other % 2, c), device_id_type=MESH
        )

    loop(nl - 1, greet)
    pl.semaphore_wait(barrier, nl + 2)

    relations = ((sib, dev_s), (yc, dev_y), (dg, dev_g))

    class Weight:
        def __init__(self, src, dst):
            self.src, self.dst = src, dst
            self.a, self.x, self.l = sem(4), sem(4), lsem()
            self.z = sem(2 * (ndp - 1))

        def start(self):
            lc(self.src(c, None), self.dst(c, r, None), self.l).start()
            for rel, (to, dev) in enumerate(relations):
                z = None if rel == 0 else d
                cp = rc(self.src(to, z), self.dst(c, r, z), self.a + 1 + rel, dev)
                cp.start()
                finals.append(cp.wait_send)

        def spread(self):
            for rel in (1, 2):
                cs, dev = relations[rel]
                part = self.dst(cs, r, d)
                rc(part, part, self.a + 1 + rel, dev).wait_recv()
                base = self.z + (rel - 1) * (ndp - 1)

                def one(o):
                    rc(part, part, base + o, ((d + o + 1) % ndp, r, c)).start()

                loop(ndp - 1, one)

        def forward(self, rel):
            if rel == -1:
                self.hand(self.src(c, None), c, rel)
                return
            cs, dev = relations[rel]
            if rel == 0:
                here = self.dst(cs, r, None)
                rc(here, here, self.a + 1, dev).wait_recv()
            else:
                base = self.z + (rel - 1) * (ndp - 1)

                def one(o):
                    part = self.dst(cs, r, (d + ndp - o - 1) % ndp)
                    rc(part, part, base + o, ((d + o + 1) % ndp, r, c)).wait()

                loop(ndp - 1, one)
            self.hand(self.dst(cs, r, None), cs, rel)

        def hand(self, block, cs, rel):
            cp = rc(block, self.dst(cs, r, None), self.x + 1 + rel, dev_x)
            cp.start()
            finals.append(cp.wait_send)

        def wait_own(self):
            lc(self.src(c, None), self.dst(c, r, None), self.l).wait()

        def wait_other(self):
            for rel, cs in enumerate((c, sib, yc, dg)):
                there = self.dst(cs, q_, None)
                rc(there, there, self.x + rel, dev_x).wait_recv()

    def part(start, size, z):
        if z is None:
            return at(start, size)
        return at(start + z * (size // ndp), size // ndp)

    w_qkv = Weight(
        lambda c2, z: wqkv.at[:, part(0, 256, z), at(c2 * 128, 128)],
        lambda cs, ro, z: WQ.at[:, part(cs * 256, 256, z), at(ro * 128, 128)],
    )
    w_fc1 = Weight(
        lambda c2, z: wfc1.at[part(0, 256, z), at(c2 * 512, 512)],
        lambda cs, ro, z: WF1.at[part(cs * 256, 256, z), at(ro * 512, 512)],
    )
    w_fc2 = Weight(
        lambda c2, z: wfc2.at[part(c2 * 512, 512, z), :],
        lambda cs, ro, z: WF2.at[part(ro * 512, 512, z), at(cs * 256, 256)],
    )
    phase("p01_wsend")
    w_qkv.start()
    w_qkv.forward(-1)

    SBX[r, 0:1, :] = bfc1[...]
    SBX[r, 1:2, 0:128] = bqv[0:1, :]
    SBX[r, 1:2, 128:256] = bqv[1:2, :]
    sbx = sem()
    cp = rc(SBX.at[r], SBX.at[r], sbx, dev_x)
    cp.start()
    finals.append(cp.wait_send)

    wo, wol = sem(4), lsem(4)

    def start_wout():
        for cs in range(4):
            place = WOUT.at[at(256 * cs + 128 * r, 128), :]
            cp = rc(wout.at[at(cs * 128, 128), :], place, wo + cs, dev_x)
            cp.start()
            finals.append(cp.wait_send)
            lc(wout.at[at(cs * 128, 128), :], place, wol + cs).start()

    def wait_wout():
        for cs in range(4):
            place = WOUT.at[at(256 * cs + 128 * r, 128), :]
            lc(wout.at[at(cs * 128, 128), :], place, wol + cs).wait()
            there = WOUT.at[at(256 * cs + 128 * q_, 128), :]
            rc(there, there, wo + cs, dev_x).wait_recv()

    class ToAll:
        def __init__(self, buf):
            self.buf, self.s = buf, sem(nl - 1)

        def start(self):
            def one(o):
                other = (me + o + 1) % nl
                rc(self.buf.at[me], self.buf.at[me], self.s + o, (other // 2, other % 2, c)).start()

            loop(nl - 1, one)

        def wait(self):
            def one(o):
                other = (me + nl - o - 1) % nl
                rc(self.buf.at[other], self.buf.at[other], self.s + o, dev_x).wait()

            loop(nl - 1, one)

    class Gather:
        def __init__(self, buf):
            self.buf, self.s = buf, sem(12)
            finals.append(lambda: loop(4, self.drain))

        def reg(self, i, cs):
            return self.buf.at[rows_of(i, 256), at(cs * 256, 256)]

        def start(self, i):
            mine = self.reg(i, c)
            rc(mine, mine, self.s + i, dev_y).start()
            rc(mine, mine, self.s + 4 + i, dev_s).start()

        def forward(self, i):
            theirs = self.reg(i, yc)
            rc(theirs, theirs, self.s + i, dev_y).wait_recv()
            rc(theirs, theirs, self.s + 8 + i, dev_s).start()

        def wait(self, i):
            a, b = self.reg(i, sib), self.reg(i, dg)
            rc(a, a, self.s + 4 + i, dev_s).wait_recv()
            rc(b, b, self.s + 8 + i, dev_s).wait_recv()

        def drain(self, i):
            mine, theirs = self.reg(i, c), self.reg(i, yc)
            rc(mine, mine, self.s + i, dev_y).wait_send()
            rc(mine, mine, self.s + 4 + i, dev_s).wait_send()
            rc(theirs, theirs, self.s + 8 + i, dev_s).wait_send()

    class Scatter:
        def __init__(self, part, snd, srec, ysnd, yrec, acc):
            self.part, self.snd, self.srec = part, snd, srec
            self.ysnd, self.yrec, self.acc = ysnd, yrec, acc
            self.s = sem(8)

        def one(self, i):
            rows = rows_of(i, 256)
            self.snd[rows, 0:256] = self.part(i, dg).astype(bf16)
            self.snd[rows, 256:512] = self.part(i, sib).astype(bf16)
            rc(self.snd.at[rows], self.srec.at[rows], self.s + i, dev_s).start()

        def two(self, i):
            rows = rows_of(i, 256)
            value = self.part(i, yc)
            rc(self.snd.at[rows], self.srec.at[rows], self.s + i, dev_s).wait_recv()
            self.ysnd[rows, :] = (value + self.srec[rows, 0:256].astype(f32)).astype(bf16)
            rc(self.ysnd.at[rows], self.yrec.at[rows], self.s + 4 + i, dev_y).start()

        def three(self, i):
            rows = rows_of(i, 256)
            self.acc[rows, :] = self.part(i, c) + self.srec[rows, 256:512].astype(f32)

        def four(self, i):
            rows = rows_of(i, 256)
            rc(self.ysnd.at[rows], self.yrec.at[rows], self.s + 4 + i, dev_y).wait_recv()
            return self.acc[rows, :] + self.yrec[rows, :].astype(f32)

        def drain(self):
            def one(i):
                rows = rows_of(i, 256)
                rc(self.snd.at[rows], self.srec.at[rows], self.s + i, dev_s).wait_send()
                rc(self.ysnd.at[rows], self.yrec.at[rows], self.s + 4 + i, dev_y).wait_send()

            loop(4, one)

        def launch(self):
            loop(4, self.one)
            loop(4, self.two)
            loop(4, self.three)

    class Stats:
        def __init__(self, e):
            self.e, self.s = e, sem(3)

        def put(self, i, a, b):
            both = jnp.where(lane128 == 0, a, jnp.where(lane128 == 1, b, 0.0)).T
            ST[self.e, c, pl.ds(i, 1), :] = both[0:1, :]
            ST[self.e, c, pl.ds(8 + i, 1), :] = both[1:2, :]

        def exchange(self):
            mine = ST.at[self.e, c]
            for n, dev in enumerate((dev_s, dev_y, dev_g)):
                cp = rc(mine, mine, self.s + n, dev)
                cp.start()
                finals.append(cp.wait_send)

        def total(self):
            for n, (dev, cs) in enumerate(((dev_s, sib), (dev_y, yc), (dev_g, dg))):
                there = ST.at[self.e, cs]
                rc(there, there, self.s + n, dev).wait_recv()
            total = ST[self.e, 0] + ST[self.e, 1] + ST[self.e, 2] + ST[self.e, 3]
            return total[0:8, :], total[8:16, :]

    def column(n, i):
        half = jnp.broadcast_to(CV[n, pl.ds(i, 1), :], (128, 128)).T
        return jnp.concatenate([half, half], axis=1)

    def token_sum(value):
        return jnp.sum(value, axis=0, keepdims=True)

    def shift(k):
        return mod[3 * k - 3 : 3 * k - 2, :]

    def scale(k):
        return 1.0 + mod[3 * k - 2 : 3 * k - 1, :]

    def gate(k):
        return mod[3 * k - 1 : 3 * k, :]

    mine = at(256 * c, 256)
    SVL[...] = jnp.zeros_like(SVL)
    G_SHIFT1, G_SCALE1, G_GATE1 = (2, 0), (2, 256), (3, 0)
    G_SHIFT2, G_SCALE2, G_GATE2 = (3, 256), (4, 0), (4, 256)

    def add_to(where, value):
        row, lane = where
        SVL[row : row + 1, lane : lane + value.shape[1]] += value

    phase("p02_n1")
    ACA[me] = actb[...]
    aca = ToAll(ACA)
    st1, st2, st3, st4 = Stats(0), Stats(1), Stats(2), Stats(3)
    cx.wait()

    def n1_sums(i):
        x = X[rows_of(i, 128), :]
        st1.put(i, jnp.sum(x, axis=1, keepdims=True), jnp.sum(x * x, axis=1, keepdims=True))

    loop(8, n1_sums)
    st1.exchange()
    w_qkv.forward(0)
    ccot.wait()

    def gm_step(i):
        rows = rows_of(i, 128)
        g = COT[rows, :] * gate(2)
        add_to((6, 256), token_sum(g))
        GM[rows, mine] = g.astype(bf16)

    loop(8, gm_step)
    w_qkv.spread()
    phase("p03_n1stat")
    s1, s2 = st1.total()
    average = s1 / D
    CV[0] = average
    CV[1] = lax.rsqrt(s2 / D - average * average + EPSILON)
    ag_h1, ag_mix, ag_h2, ag_gm = Gather(H1), Gather(MIX), Gather(H2), Gather(GM)

    def n1_norm(i):
        for s in range(2):
            rows = at(i * 256 + s * 128, 128)
            normed = (X[rows, :] - column(0, 2 * i + s)) * column(1, 2 * i + s)
            N1[rows, :] = normed
            H1[rows, mine] = (normed * scale(1) + shift(1)).astype(bf16)
        ag_h1.start(i)

    phase("p04_n1norm")
    loop(4, n1_norm)
    phase("p05_wqkvfwd")
    w_fc1.start()
    w_fc2.start()
    ag_gm.start(0)
    ag_gm.start(1)
    w_qkv.forward(1)
    w_qkv.forward(2)
    start_wout()
    w_fc1.forward(-1)
    w_fc1.forward(0)
    w_fc2.forward(-1)
    w_fc2.forward(0)
    phase("p06_h1fwd")
    loop(4, ag_h1.forward)
    phase("p07_wqkvwait")
    there = SBX.at[q_]
    rc(there, there, sbx, dev_x).wait_recv()
    w_qkv.wait_own()
    w_qkv.wait_other()

    def qkv_step(i):
        ag_h1.wait(i)
        rows = rows_of(i, 256)
        h = H1[rows, :]
        qb = jnp.concatenate([SBX[0, 1:2, 0:128], SBX[1, 1:2, 0:128]], axis=1)
        vb = jnp.concatenate([SBX[0, 1:2, 128:256], SBX[1, 1:2, 128:256]], axis=1)
        Q[rows, :] = (dot(h, WQ[0], NN) + qb).astype(bf16)
        K[rows, :] = dot(h, WQ[1], NN).astype(bf16)
        V[rows, :] = (dot(h, WQ[2], NN) + vb).astype(bf16)

    phase("p08_qkv")
    loop(4, qkv_step)

    def att_step(i):
        rows = rows_of(i, 256)
        qt = Q[rows, :]
        out = jnp.zeros((256, 256), f32)
        logs = jnp.zeros((256, 128), f32)
        lane = lax.broadcasted_iota(jnp.int32, (256, 128), 1)
        for h in range(4):
            qm = jnp.where(lane256 == h, qt, jnp.zeros_like(qt))
            s = dot(qm, K[...], NT)
            m = jnp.max(s, axis=1, keepdims=True)
            p = jnp.exp2((s - m) * (FACTOR * LOG2E))
            total = jnp.sum(p, axis=1, keepdims=True)
            o = dot(p.astype(bf16), V[...], NN)
            out = jnp.where(lane256 == h, o / total, out)
            logs = jnp.where(lane == h, m * (FACTOR * LOG2E) + jnp.log2(total), logs)
        MIX[rows, mine] = out.astype(bf16)
        LT[rows, :] = logs
        ag_mix.start(i)

    w_fc1.spread()
    w_fc2.spread()
    aca.start()
    phase("p09_att")
    loop(4, att_step)
    phase("p10_fc1fwd")
    ag_gm.start(2)
    ag_gm.start(3)
    for rel in (1, 2):
        w_fc1.forward(rel)
    for rel in (1, 2):
        w_fc2.forward(rel)
    phase("p11_mixfwd")
    ag_gm.forward(0)
    ag_gm.forward(1)
    loop(4, ag_mix.forward)

    phase("p12_woutwait")
    wait_wout()

    def out_step(i):
        ag_mix.wait(i)
        rows = rows_of(i, 256)
        att = dot(MIX[rows, :], WOUT[...], NN) + bout[...]
        ATT[rows, :] = att
        X[rows, :] = X[rows, :] + gate(1) * att

    phase("p13_outproj")
    loop(4, out_step)

    def n2_sums(i):
        x = X[rows_of(i, 128), :]
        st2.put(i, jnp.sum(x, axis=1, keepdims=True), jnp.sum(x * x, axis=1, keepdims=True))

    phase("p14_n2sums")
    loop(8, n2_sums)
    st2.exchange()
    ag_gm.forward(2)
    ag_gm.forward(3)
    phase("p15_n2stat")
    s1, s2 = st2.total()
    average = s1 / D
    CV[2] = average
    CV[3] = lax.rsqrt(s2 / D - average * average + EPSILON)

    def n2_norm(i):
        for s in range(2):
            rows = at(i * 256 + s * 128, 128)
            normed = (X[rows, :] - column(2, 2 * i + s)) * column(3, 2 * i + s)
            N2[rows, :] = normed
            H2[rows, mine] = (normed * scale(2) + shift(2)).astype(bf16)
        ag_h2.start(i)

    phase("p16_n2norm")
    loop(4, n2_norm)
    phase("p19_h2fwd")
    loop(4, ag_h2.forward)
    w_fc1.wait_own()
    w_fc2.wait_own()

    def mlp_step(half, units):
        def step(i):
            rows = rows_of(i, 256)
            v = dot(H2[rows, :], WF1[:, units], NN) + SBX[half, 0:1, :]
            g = dot(GM[rows, :], WF2[units, :], NT)
            sq = v * v
            t = jnp.tanh(GC * v * (1.0 + 0.044715 * sq))
            hf = 0.5 * (1.0 + t)
            ACT[rows, units] = (v * hf).astype(bf16)
            slope = hf + (0.5 * GC) * v * (1.0 - t * t) * (1.0 + (3 * 0.044715) * sq)
            g = g * slope
            SVL[pl.ds(half, 1), :] += token_sum(g)
            GPRE[rows, units] = g.astype(bf16)

        return step

    loop(4, ag_gm.wait)
    loop(4, ag_h2.wait)
    phase("p20_mlp0")
    loop(4, mlp_step(r, at(512 * r, 512)))
    phase("p21_fcwait")
    w_fc1.wait_other()
    w_fc2.wait_other()
    phase("p21_mlp1")
    loop(4, mlp_step(q_, at(512 * q_, 512)))

    rs_h2 = Scatter(
        lambda i, b: dot(GPRE[rows_of(i, 256), :], WF1[at(b * 256, 256), :], NT),
        SA, SAR, YA, YAR, ACCA,
    )
    phase("p22_rsh2")
    rs_h2.launch()

    x1, x2, xq, xo = sem(4), sem(4), sem(3), sem()

    half = ndp // 2
    upper = d >= half
    inward = jnp.where(upper, d - 1, d + 1)
    outward = jnp.where(upper, (d + 1) % ndp, (d + ndp - 1) % ndp)
    pos = jnp.where(upper, ndp - 1 - d, d)
    dev_in, dev_out = (inward, r, c), (outward, r, c)

    class Piece:
        def __init__(self, plan, xsend, xrecv, xs, send, recv, across, regions, steps, block, place):
            self.plan = list(plan)
            self.xsend, self.xrecv, self.xs = xsend, xrecv, xs
            self.send, self.recv, self.across, self.regions = send, recv, across, regions
            self.steps, self.block, self.place = steps, block, place
            self.s, self.c, self.g, self.a, self.l = sem(), sem(), sem(len(regions)), sem(4), lsem()
            self.state = 0

        def add(self, other):
            count_, cut = self.steps

            def one(i):
                k = cut(i)
                self.send[k] = (self.send[k].astype(f32) + other[k].astype(f32)).astype(bf16)

            loop(count_, one)

        def spread(self):
            lc(self.block(c), self.place(c), self.l).start()
            if self.a is not None:
                for rel, (to, dev) in enumerate(relations):
                    rc(self.block(to), self.place(c), self.a + rel, dev).start()

        def spread_wait(self):
            lc(self.block(c), self.place(c), self.l).wait()
            if self.a is not None:
                for rel, (cs, dev) in enumerate(relations):
                    rc(self.block(cs), self.place(cs), self.a + rel, dev).wait()
            for n, region in enumerate(self.regions):
                rc(region, region, self.g + n, dev_out).start()

        def step(self):
            k = self.state
            self.state += 1
            up = rc(self.send, self.recv, self.s, dev_in)
            cross = rc(self.send, self.across, self.c, dev_in)
            if k == 0:
                rc(self.xsend, self.xrecv, self.xs, dev_x).wait()
                self.add(self.xrecv)
                for t in range(half - 1):

                    @pl.when(pos == t)
                    def _():
                        if t > 0:
                            up.wait_recv()
                            self.add(self.recv)
                        up.start()

            elif k == 1:

                @pl.when(pos == half - 1)
                def _():
                    up.wait_recv()
                    self.add(self.recv)
                    cross.start()

            elif k == 2:

                @pl.when(pos == half - 1)
                def _():
                    cross.wait()
                    self.add(self.across)
                    self.spread()

            elif k == 3:
                pl.when(pos == half - 1)(self.spread_wait)
            else:
                outs = [rc(a, a, self.g + n, dev_out) for n, a in enumerate(self.regions)]

                for t in range(half - 2, -1, -1):

                    @pl.when(pos == t)
                    def _():
                        for out in outs:
                            out.wait_recv()
                            if t > 0:
                                out.start()

                @pl.when(pos > 0)
                def _():
                    for out in outs:
                        out.wait_send()

                pl.when(pos < half - 1)(up.wait_send)

    pieces = []
    for n in range(4):
        k = (n // 2, slice(None), pl.ds(128 * (n % 2), 128), slice(None))
        pieces.append(
            Piece(
                PLAN[n],
                X1S.at[k], X1R.at[k], x1 + n, ZS1.at[k], ZR1.at[k], ZC1.at[k],
                [g1_o.at[k[2], pl.ds(512 * cs + 256 * k[0], 256)] for cs in range(4)], (4, lambda i: i),
                lambda c2, k=k: ZS1.at[k[0], c2, k[2], :],
                lambda cs, k=k: g1_o.at[k[2], at(cs * 512 + 256 * k[0], 256)],
            )
        )
    for n in range(4):
        b = pl.ds(128 * n, 128)
        pieces.append(
            Piece(
                PLAN[4 + n],
                X2S.at[b], X2R.at[b], x2 + n, ZS2.at[b], ZR2.at[b], ZC2.at[b],
                [g2_o.at[:, b, :]], (4, lambda i: (rows_of(i, 32), slice(None))),
                lambda c2, b=b: ZS2.at[b, at(256 * c2, 256)],
                lambda cs, b=b: g2_o.at[cs, b, :],
            )
        )
    piece_o = Piece(
        PLAN[8],
        XOS, XOR, xo, ZSO, ZRO, ZCO,
        [go_o], (4, lambda i: (rows_of(i, 128), slice(None))),
        lambda c2: ZSO, lambda cs: go_o,
    )
    piece_o.a = None
    pieces.append(piece_o)
    for n in range(3):
        pieces.append(
            Piece(
                PLAN[9 + n],
                XQS.at[n], XQR.at[n], xq + n, ZSQ.at[n], ZRQ.at[n], ZCQ.at[n],
                [gq_o.at[n]], (4, lambda i: i),
                lambda c2, n=n: ZSQ.at[n, c2],
                lambda cs, n=n: gq_o.at[n, :, at(128 * cs, 128)],
            )
        )

    def tick(now):
        due = sorted((p.plan[k], n, k) for n, p in enumerate(pieces) for k in range(p.state, 4) if p.plan[k] <= now)
        for _, n, k in due:
            assert pieces[n].state == k
            if now > 900:
                phase(f"p52_{n:02d}_{k}")
            pieces[n].step()

    def dw1_half(p):
        def step(i):
            h = H2[:, rows_of(i, 256)]
            X1S[p, i] = dot(h, GPRE[:, at(512 * q_ + 256 * p, 256)], TN).astype(bf16)
            ZS1[p, i] = dot(h, GPRE[:, at(512 * r + 256 * p, 256)], TN).astype(bf16)

        loop(4, step)
        for n in range(2):
            b = pl.ds(128 * n, 128)
            rc(X1S.at[p, :, b, :], X1R.at[p, :, b, :], x1 + 2 * p + n, dev_x).start()

    phase("p23_dw1")
    dw1_half(0)
    dw1_half(1)

    rs_out = Scatter(
        lambda i, b: dot(ACT[rows_of(i, 256), :], WF2[:, at(b * 256, 256)], NN),
        SC, SCR, YC, YCR, ACCA,
    )

    def dw2_step(i):
        rows = rows_of(i, 256)
        X2S[rows, :] = dot(ACT[:, at(512 * q_ + 256 * i, 256)], GM[...], TN).astype(bf16)
        for n in range(2):
            block = at(256 * i + 128 * n, 128)
            rc(X2S.at[block], X2R.at[block], x2 + 2 * i + n, dev_x).start()
        ZS2[rows, :] = dot(ACT[:, at(512 * r + 256 * i, 256)], GM[...], TN).astype(bf16)

    phase("p25_dw2")
    loop(2, dw2_step)
    tick(92)

    def b2_sums(i):
        value = rs_h2.four(i)
        ACCA[rows_of(i, 256), :] = value
        for s in range(2):
            rows = at(i * 256 + s * 128, 128)
            gh, normed = ACCA[rows, :], N2[rows, :]
            add_to(G_SHIFT2, token_sum(gh))
            hn = gh * normed
            add_to(G_SCALE2, token_sum(hn))
            st3.put(
                2 * i + s,
                jnp.sum(gh * scale(2), axis=1, keepdims=True),
                jnp.sum(hn * scale(2), axis=1, keepdims=True),
            )

    phase("p26_b2sums")
    loop(4, b2_sums)
    st3.exchange()
    phase("p27_b2stat")
    s1, s2 = st3.total()
    CV[4] = s1 / D
    CV[5] = s2 / D

    def b2_back(i):
        rows = rows_of(i, 128)
        inner = ACCA[rows, :] * scale(2) - column(4, i) - N2[rows, :] * column(5, i)
        gmid = COT[rows, :] + column(3, i) * inner
        N2[rows, :] = gmid
        ga = gmid * gate(1)
        add_to((6, 0), token_sum(ga))
        add_to(G_GATE1, token_sum(gmid * ATT[rows, :]))
        GA[rows, :] = ga.astype(bf16)

    def out_done(i):
        value = rs_out.four(i) + bfc2[...]
        rows = rows_of(i, 256)
        add_to(G_GATE2, token_sum(COT[rows, :] * value))
        X[rows, :] = X[rows, :] + gate(2) * value

    phase("p29_b2back")
    loop(8, b2_back)
    tick(97)
    rs_mix = Scatter(
        lambda i, b: dot(GA[rows_of(i, 256), :], WOUT[at(b * 256, 256), :], NT),
        SC, SCR, YC, YCR, ACCA,
    )
    phase("p30_rsmix")
    loop(4, rs_mix.one)
    loop(4, rs_mix.two)
    tick(100)
    loop(4, rs_mix.three)

    def dwo_step(i):
        rows = rows_of(i, 128)
        XOS[rows, :] = dot(MIX[:, at(256 * i + 128 * q_, 128)], GA[...], TN).astype(bf16)
        ZSO[rows, :] = dot(MIX[:, at(256 * i + 128 * r, 128)], GA[...], TN).astype(bf16)

    phase("p31_dwo")
    loop(4, dwo_step)
    rc(XOS, XOR, xo, dev_x).start()
    tick(103)

    def do_step(i):
        DO[rows_of(i, 256), :] = rs_mix.four(i).astype(bf16)

    def inner_step(i):
        rows = rows_of(i, 128)
        prod = DO[rows, :].astype(f32) * MIX[rows, mine].astype(f32)
        lane = lax.broadcasted_iota(jnp.int32, (128, 256), 1) // HD
        inner = jnp.zeros((128, 128), f32)
        for h in range(4):
            one = jnp.sum(jnp.where(lane == h, prod, 0.0), axis=1, keepdims=True)
            inner = jnp.where(lane128 == h, one, inner)
        I8[:, rows] = inner.T[0:8, :]
        L8[:, rows] = LT[rows, :].T[0:8, :]

    def kt_step(i):
        rows = rows_of(i, 256)
        KT[:, rows] = K[rows, :].astype(f32).T.astype(bf16)

    phase("p33_kt")
    loop(4, kt_step)
    BQV[...] = jnp.zeros_like(BQV)
    phase("p34_do")
    for i in range(4):
        do_step(i)
        tick(105 + 2.5 * i)
    phase("p35_inner")
    loop(8, inner_step)
    lane_all = lax.broadcasted_iota(jnp.int32, (1024, 256), 1) // HD

    def head_back(n, half, now):
        h = 2 * half + n
        QM[...] = jnp.where(lane_all == h, Q[...], jnp.zeros_like(Q[...]))
        DOM[...] = jnp.where(lane_all == h, DO[...], jnp.zeros_like(DO[...]))
        feats = at(h * HD, HD)
        lanes = at(half * 128, 128)

        def step(i, first):
            rows = rows_of(i, 512)
            p = jnp.exp2(dot(K[rows, :], QM[...], NT) * (FACTOR * LOG2E) - L8[pl.ds(h, 1), :])
            dp = dot(V[rows, :], DOM[...], NT)
            ds = (p * (dp - I8[pl.ds(h, 1), :])).astype(bf16)
            gv = dot(p.astype(bf16), DOM[:, lanes], NN)
            gk = dot(ds, QM[:, lanes], NN)
            if n == 0:
                DV[rows, lanes] = gv
                DK[rows, lanes] = gk
            else:
                DV[rows, lanes] += gv
                DK[rows, lanes] += gk
            gq = dot(KT[feats, rows], ds, NN)

            if first:
                DQT[feats, :] = gq
            else:
                DQT[feats, :] += gq

        step(0, True)
        step(1, False)
        tick(now)

    def gqkv_half(half):
        feats, lanes = at(128 * half, 128), at(128 * half, 128)

        def step(i):
            rows = rows_of(i, 256)
            gq = DQT[feats, rows].T * FACTOR
            gk, gv = DK[rows, lanes] * FACTOR, DV[rows, lanes]
            BQV[half, 0:1, :] += token_sum(gq)
            BQV[half, 1:2, :] += token_sum(gv)
            GQKV[0, rows, lanes] = gq.astype(bf16)
            GQKV[1, rows, lanes] = gk.astype(bf16)
            GQKV[2, rows, lanes] = gv.astype(bf16)

        loop(4, step)

    def dwq_half(half, out, j):
        lanes = at(128 * half, 128)

        def step(i):
            out[j, i] = dot(H1[:, rows_of(i, 256)], GQKV[j, :, lanes], TN).astype(bf16)

        loop(4, step)

    phase("p36_head0")
    head_back(0, q_, 116)
    tick(117.5)
    phase("p36_head1")
    head_back(1, q_, 119)
    gqkv_half(q_)
    phase("p37_dwq0")
    for j in range(3):
        dwq_half(q_, XQS, j)
        rc(XQS.at[j], XQR.at[j], xq + j, dev_x).start()
        tick(122.5 + 1.5 * j)
    phase("p38_head2")
    head_back(0, r, 127)
    tick(128.5)
    phase("p39_head3")
    head_back(1, r, 130)
    gqkv_half(r)
    tick(131.5)

    def part_h1(i, b):
        rows, feats = rows_of(i, 256), at(b * 256, 256)
        total = dot(GQKV[0, rows, :], WQ[0, feats, :], NT)
        total = total + dot(GQKV[1, rows, :], WQ[1, feats, :], NT)
        return total + dot(GQKV[2, rows, :], WQ[2, feats, :], NT)

    phase("p43_rsh1")
    rs_h2.drain()
    rs_h1 = Scatter(part_h1, SA, SAR, YA, YAR, ACCA)
    loop(4, rs_h1.one)
    loop(4, rs_h1.two)
    phase("p44_three")
    loop(4, rs_h1.three)
    tick(136)
    phase("p44_dwq1")
    for j in range(3):
        dwq_half(r, ZSQ, j)
        tick(138 + 1.5 * j)

    def b1_sums(i):
        value = rs_h1.four(i)
        ACCA[rows_of(i, 256), :] = value
        for s in range(2):
            rows = at(i * 256 + s * 128, 128)
            gh, normed = ACCA[rows, :], N1[rows, :]
            add_to(G_SHIFT1, token_sum(gh))
            hn = gh * normed
            add_to(G_SCALE1, token_sum(hn))
            st4.put(
                2 * i + s,
                jnp.sum(gh * scale(1), axis=1, keepdims=True),
                jnp.sum(hn * scale(1), axis=1, keepdims=True),
            )

    phase("p48_b1sums")
    for i in range(4):
        b1_sums(i)
        tick(142.5 + 1.5 * i)
    st4.exchange()
    phase("p50_b1stat")
    s1, s2 = st4.total()
    CV[6] = s1 / D
    CV[7] = s2 / D

    def b1_back(i):
        rows = rows_of(i, 128)
        inner = ACCA[rows, :] * scale(1) - column(6, i) - N1[rows, :] * column(7, i)
        N2[rows, :] = N2[rows, :] + column(1, i) * inner

    phase("p51_b1back")
    loop(8, b1_back)
    put_grad = lc(N2, gin_o, lsem())
    put_grad.start()
    finals.append(put_grad.wait)
    tick(151)
    phase("p51_rsout")
    rs_mix.drain()
    loop(4, rs_out.one)
    loop(4, rs_out.two)
    loop(4, rs_out.three)
    tick(153)
    tick(156)
    for i in range(4):
        out_done(i)
        tick(158 + 2.5 * i)
    put_result = lc(X, res_o, lsem())
    put_result.start()
    finals.append(put_result.wait)
    SVL[5:6, 0:128] = BQV[0, 0:1, :]
    SVL[5:6, 128:256] = BQV[1, 0:1, :]
    SVL[5:6, 256:384] = BQV[0, 1:2, :]
    SVL[5:6, 384:512] = BQV[1, 1:2, :]
    SVA[me] = SVL[...]
    sva = ToAll(SVA)
    sva.start()

    phase("p52_ticks")
    tick(1000)

    phase("p56_sva")
    aca.wait()
    sva.wait()
    total = jnp.zeros((8, 512), f32)
    for l in range(nl):
        one = SVA[l]
        total = total + one
        act_o[l] = ACA[l]
        for k in range(6):
            gm_o[l, k : k + 1, :] = one[2 + k // 2 : 3 + k // 2, 256 * (k % 2) : 256 * (k % 2) + 256]
        gm_o[l, 6:8, :] = jnp.zeros((2, 256), f32)
    gmo_o[...] = gm_o[me]
    first = r == 0
    for k in range(6):
        gbada_o[k : k + 1, :] = total[2 + k // 2 : 3 + k // 2, 256 * (k % 2) : 256 * (k % 2) + 256]
    gbfc1_o[...] = jnp.where(first, total[0:1, :], total[1:2, :])
    gbqv_o[0:1, :] = jnp.where(first, total[5:6, 0:128], total[5:6, 128:256])
    gbqv_o[1:2, :] = jnp.where(first, total[5:6, 256:384], total[5:6, 384:512])
    gbout_o[...] = total[6:7, 0:256]
    gbfc2_o[...] = total[6:7, 256:512]

    phase("p57_finals")
    rs_out.drain()
    rs_h1.drain()
    for one in finals:
        one()
    phase("p58_pieces")
    for n, one in enumerate(pieces):
        phase(f"p59_{n:02d}")
        one.step()
    phase("")


def call_mega(ndp, *args):
    nl = 2 * ndp
    s = jax.ShapeDtypeStruct
    vmem = pl.BlockSpec(memory_space=pltpu.VMEM)
    hbm = pl.BlockSpec(memory_space=pl.ANY)
    outs = (
        (s((T, 256), f32), hbm),
        (s((T, 256), f32), hbm),
        (s((3, 256, 512), bf16), hbm),
        (s((512, 256), bf16), hbm),
        (s((256, 2048), bf16), hbm),
        (s((4, 512, 256), bf16), hbm),
        (s((nl, 8, 256), f32), vmem),
        (s((nl, 8, 128), f32), vmem),
        (s((8, 256), f32), vmem),
        (s((2, 128), f32), vmem),
        (s((1, 512), f32), vmem),
        (s((1, 256), f32), vmem),
        (s((1, 256), f32), vmem),
        (s((6, 256), f32), vmem),
    )

    def v(*shape, t=bf16):
        return pltpu.VMEM(shape, t)

    scratch = (
        [v(T, 256, t=f32)] * 5
        + [v(3, D, 256), v(D, 256), v(D, D), v(D, D)]
        + [v(T, D)] * 4
        + [v(T, 256)] * 3
        + [v(256, T), v(T, 128, t=f32), v(8, T, t=f32), v(8, T, t=f32)]
        + [v(T, 256)]
        + [v(T, D)] * 2
        + [v(T, 512), v(T, 512), v(T, 256), v(T, 256)] * 2
        + [v(T, 256, t=f32)]
        + [v(256, T, t=f32), v(T, 256, t=f32), v(T, 256, t=f32), v(T, 256), v(T, 256), v(3, T, 256)]
        + [v(2, 4, 256, 256)] * 5
        + [v(512, D)] * 5
        + [v(3, 4, 256, 128)] * 5
        + [v(512, 256)] * 5
        + [v(4, 4, 16, 128, t=f32), v(8, 8, 128, t=f32), v(2, 8, 512, t=f32), v(8, 512, t=f32)]
        + [v(nl, 8, 512, t=f32), v(nl, 8, 128, t=f32), v(2, 8, 128, t=f32)]
        + [pltpu.SemaphoreType.DMA((N_SEM + 16 * ndp,))] * 2
        + [pltpu.SemaphoreType.DMA((40,))]
    )
    return pl.pallas_call(
        functools.partial(mega, ndp),
        out_shape=[o[0] for o in outs],
        in_specs=[hbm] * 6 + [vmem] * 6,
        out_specs=[o[1] for o in outs],
        scratch_shapes=scratch,
        name="block",
        compiler_params=pltpu.CompilerParams(
            collective_id=0, has_side_effects=True, vmem_limit_bytes=67043328
        ),
    )(*args)


def body(
    inputs, cond, w_ada, b_ada, w_qkv, b_qv, w_out, b_out, w_fc1, b_fc1, w_fc2, b_fc2, cotangent
):
    assert cond.shape[0] == 1 and inputs.shape == (T, 256)
    ndp = lax.axis_size("dp")
    act_cond = jax.nn.silu(cond).astype(bf16)
    modulation = (
        jnp.einsum("sd,dke->ske", act_cond, w_ada, preferred_element_type=f32) + b_ada[None]
    )[0]
    mod8 = jnp.concatenate([modulation, jnp.zeros((2, 256), f32)], axis=0)
    actb = act_cond.astype(f32).reshape(8, 128)
    (
        result, grad_inputs, gq, go, g1, g2, gm, act_all, gmo, gbqv, gbfc1, gbout, gbfc2, gbada,
    ) = call_mega(
        ndp, inputs, cotangent, w_qkv, w_out, w_fc1, w_fc2, mod8, actb,
        b_qv, b_out[None], b_fc1[None], b_fc2[None],
    )
    grad_w_ada = jnp.einsum(
        "ld,lke->dke", act_all.reshape(-1, D), gm[:, :6], precision=lax.Precision.HIGHEST,
        preferred_element_type=f32,
    )
    grad_silu = lax.psum(
        jnp.einsum(
            "ke,dke->d", gmo[:6], w_ada.astype(f32), precision=lax.Precision.HIGHEST,
            preferred_element_type=f32,
        )[None],
        "col",
    )
    grad_cond = jax.vjp(jax.nn.silu, cond)[1](grad_silu)[0]
    return (
        result,
        grad_inputs,
        grad_cond,
        grad_w_ada,
        gbada,
        gq.astype(f32),
        gbqv,
        go.astype(f32),
        gbout[0],
        g1.astype(f32),
        gbfc1[0],
        g2.reshape(2048, 256).astype(f32),
        gbfc2[0],
    )


def solution(mesh):
    return jax.shard_map(
        body,
        mesh=mesh,
        in_specs=(
            P(("dp", "row"), "col"),
            P(("dp", "row"), None),
            P(None, None, "col"),
            P(None, "col"),
            P(None, "col", "row"),
            P(None, ("row", "col")),
            P("row", "col"),
            P("col"),
            P("col", "row"),
            P(("row", "col")),
            P("row", "col"),
            P("col"),
            P(("dp", "row"), "col"),
        ),
        out_specs=(
            P(("dp", "row"), "col"),
            P(("dp", "row"), "col"),
            P(("dp", "row"), None),
            P(None, None, "col"),
            P(None, "col"),
            P(None, "col", "row"),
            P(None, ("row", "col")),
            P("row", "col"),
            P("col"),
            P("col", "row"),
            P(("row", "col")),
            P("row", "col"),
            P("col"),
        ),
        check_vma=False,
    )
```

time: 320 us -> 253 us (0.79)
  Pallas kernels: 283 us -> 218 us
    pallas_call x1, Pallas kernels: 283 us -> 218 us  [call_mega(): pl.pallas_call(functools.partial(mega, ndp), out_shape=[o[0] for o in out...]
where the time goes in v2:
time: 253 us
  Pallas kernels  218 us (86%)
  matrix products  13.9 us (5%)
  other arithmetic  7.2 us (3%)
  local copies, waits for them, and re-layouts  6.88 us (3%)
  blocking collectives  5.93 us (2%)
    pallas_call x1, Pallas kernels, call_mega(): pl.pallas_call(functools.partial(mega, ndp), out_shape=[o[0] for o in out...  218 us
    dot_general x1, matrix products, body(): jnp.einsum('ld,lke->dke', act_all.reshape(-1, D), gm[:, :6], precision=la...  6.99 us
    psum x1, blocking collectives, body(): lax.psum(jnp.einsum('ke,dke->d', gmo[:6], w_ada.astype(f32), precision=la...  5.93 us
    unnamed x41, local copies, waits for them, and re-layouts  5.47 us

profile of v2, /device:TPU:0, one launch (start us, length us, event | category | flops | bytes accessed | tf_op | source)
XLA Modules:
  0.0 252.6 jit_solution(5786718557618897167)
XLA Ops:
  0.7 1.3 convert_convert_fusion
  2.0 0.6 copy-done.8
  2.5 2.4 fusion.5
  5.0 0.6 concatenate.3.mod
  5.6 217.9 %block.1 = (f32[1024,256]{1,0:T(8,128)}, f32[1024,256]{1,0:T(8,128)}, bf16[3,256,512]{2,1,0:T(8,128)(2,1)}, bf16[512,256]{1,0:T(8,128)(2,1)}, bf16[256,2048]{1,0...) custom-call(f32[1024,256]{1,0:T(8,128)} %x_hbm.1, ...), custom_call_target="tpu_custom_call" | custom-call | tf_op jit(solution)/shard_map/block/pallas_call | solution.py:1149
  223.5 0.0 copy-start.7
  223.5 0.0 copy-start.9
  223.5 0.0 copy-start.10
  223.5 0.0 copy-start.5
  223.5 0.0 copy-start.4
  223.5 0.8 slice_bitcast_fusion
  224.3 4.5 %convolution_bitcast_fusion = f32[1,1024]{1,0:T(1,128)S(1)} fusion(bf16[1024,6,256]{2,0,1:T(8,128)(2,1)} %param.15, f32[6,256,1]{1,0,2:T(8,128)S(1)} %slice_bitcast_fusion), kind=kOutput, calls=%fused_computation | convolution fusion | flops 18874368 | bytes 3155968 | tf_op jit(solution)/shard_map/ke,dke->d/dot_general | solution.py:1184
  228.8 5.9 %psum.7 = f32[1,1024]{1,0:T(1,128)S(1)} all-reduce(f32[1,1024]{1,0:T(1,128)S(1)} %convolution_bitcast_fusion), channel_id=1, replica_groups=mesh['dp'=4,'row'=2,'col'=4] {'col'}, use_global_device_ids=true, to_apply=%region_0.1 | all-reduce | flops 1024 | bytes 8192 | tf_op jit(solution)/shard_map/psum | solution.py:1183
  234.8 0.0 copy-done.9
  234.8 0.6 fusion.4
  235.4 0.8 convert_element_type.22
  236.2 1.4 convert_element_type.21
  237.6 0.0 copy-done.1
  237.6 1.6 convert_element_type.23
  239.2 0.0 copy-done
  239.2 1.5 bitcast_convert_fusion
  240.7 0.0 copy-done.6
  240.7 7.0 %fusion = f32[1024,6,256]{2,0,1:T(8,128)} fusion(f32[8,1024,1]{1,0,2:T(8,128)S(1)} %reshape.54, f32[8,6,256]{2,1,0:T(8,128)S(1)} %bitcast.25), kind=kOutput, calls=%fused_computation.2 | convolution fusion | flops 150994944 | bytes 6373376 | tf_op jit(solution)/shard_map/ld,lke->dke/dot_general | solution.py:1179
  247.7 0.0 copy-start.13
  247.7 0.0 copy-start.14
  247.7 1.0 copy.41
  248.7 1.0 copy.42
  249.7 0.6 copy.43
  250.3 0.6 copy.44
  250.9 0.6 copy.45
  251.4 0.6 copy.46
  252.0 0.6 copy.47
  (24 shorter events, 0.1 us)
Async XLA Ops:
  0.6 4.3 %copy-start.12 = (f32[6,256]{1,0:T(8,128)S(1)}, f32[6,256]{1,0:T(8,128)}, u32[]{:S(2)}) copy-start(f32[6,256]{1,0:T(8,128)} %param.16) | copy-start | bytes 18436
  2.0 0.6 copy-start.8
  223.5 11.3 %copy-start.7 = (f32[1,1024]{1,0:T(1,128)S(1)}, f32[1,1024]{1,0:T(1,128)}, u32[]{:S(2)}) copy-start(f32[1,1024]{1,0:T(1,128)} %param.14) | copy-start | bytes 12292
  223.5 11.3 %copy-start.9 = (f32[1,1024]{1,0:T(1,128)S(1)}, f32[1,1024]{1,0:T(1,128)}, u32[]{:S(2)}) copy-start(f32[1,1024]{1,0:T(1,128)} %copy-done.8) | copy-start | bytes 12292
  223.5 11.9 %copy-start.10 = (f32[8,8,128]{2,1,0:T(8,128)S(1)}, f32[8,8,128]{2,1,0:T(8,128)}, u32[]{:S(2)}) copy-start(f32[8,8,128]{2,1,0:T(8,128)} %get-tuple-element.30) | copy-start | bytes 98308
  223.5 11.9 %copy-start.5 = (bf16[512,256]{1,0:T(8,128)(2,1)S(1)}, bf16[512,256]{1,0:T(8,128)(2,1)}, u32[]{:S(2)}) copy-start(bf16[512,256]{1,0:T(8,128)(2,1)} %get-tuple-element.35) | copy-start | bytes 786436
  223.5 12.7 %copy-start.4 = (bf16[3,256,512]{2,1,0:T(8,128)(2,1)S(1)}, bf16[3,256,512]{2,1,0:T(8,128)(2,1)}, u32[]{:S(2)}) copy-start(bf16[3,256,512]{2,1,0:T(8,128)(2,1)} %get-tuple-element.33) | copy-start | bytes 2359300
  224.3 13.3 %copy-start.1 = (bf16[256,2048]{1,0:T(8,128)(2,1)S(1)}, bf16[256,2048]{1,0:T(8,128)(2,1)}, u32[]{:S(2)}) copy-start(bf16[256,2048]{1,0:T(8,128)(2,1)} %get-tuple-element.37) | copy-start | bytes 3145732
  235.4 3.8 %copy-start = (bf16[4,512,256]{2,1,0:T(8,128)(2,1)S(1)}, bf16[4,512,256]{2,1,0:T(8,128)(2,1)}, u32[]{:S(2)}) copy-start(bf16[4,512,256]{2,1,0:T(8,128)(2,1)} %get-tuple-element.39) | copy-start | bytes 3145732
  237.6 3.1 %copy-start.6 = (f32[8,8,256]{2,1,0:T(8,128)S(1)}, f32[8,8,256]{2,1,0:T(8,128)}, u32[]{:S(2)}) copy-start(f32[8,8,256]{2,1,0:T(8,128)} %get-tuple-element.31) | copy-start | bytes 196612
  240.7 7.0 %copy-start.3 = (f32[1024,256]{1,0:T(8,128)S(1)}, f32[1024,256]{1,0:T(8,128)}, u32[]{:S(2)}) copy-start(f32[1024,256]{1,0:T(8,128)} %get-tuple-element.56) | copy-start | bytes 3145732
  240.7 8.0 %copy-start.2 = (f32[1024,256]{1,0:T(8,128)S(1)}, f32[1024,256]{1,0:T(8,128)}, u32[]{:S(2)}) copy-start(f32[1024,256]{1,0:T(8,128)} %get-tuple-element.57) | copy-start | bytes 3145732
  247.7 2.0 copy-start.11
  247.7 2.6 %copy-start.16 = (f32[2,128]{1,0:T(2,128)S(1)}, f32[2,128]{1,0:T(2,128)}, u32[]{:S(2)}) copy-start(f32[2,128]{1,0:T(2,128)} %get-tuple-element.62) | copy-start | bytes 3076
  247.7 3.1 %copy-start.15 = (f32[1,256]{1,0:T(1,128)S(1)}, f32[1,256]{1,0:T(1,128)}, u32[]{:S(2)}) copy-start(f32[1,256]{1,0:T(1,128)} %get-tuple-element.36) | copy-start | bytes 3076
  247.7 3.7 %copy-start.13 = (f32[1,512]{1,0:T(1,128)S(1)}, f32[1,512]{1,0:T(1,128)}, u32[]{:S(2)}) copy-start(f32[1,512]{1,0:T(1,128)} %get-tuple-element.38) | copy-start | bytes 6148
  247.7 4.3 %copy-start.14 = (f32[1,256]{1,0:T(1,128)S(1)}, f32[1,256]{1,0:T(1,128)}, u32[]{:S(2)}) copy-start(f32[1,256]{1,0:T(1,128)} %get-tuple-element.40) | copy-start | bytes 3076

commit v3 on v2

--- a/solution.py
+++ b/solution.py
@@ -1176,15 +1176,26 @@
         ndp, inputs, cotangent, w_qkv, w_out, w_fc1, w_fc2, mod8, actb,
         b_qv, b_out[None], b_fc1[None], b_fc2[None],
     )
-    grad_w_ada = jnp.einsum(
-        "ld,lke->dke", act_all.reshape(-1, D), gm[:, :6], precision=lax.Precision.HIGHEST,
-        preferred_element_type=f32,
-    )
+    parts = []
+    rest = gm[:, :6]
+    for _ in range(3):
+        parts.append(lax.reduce_precision(rest, 8, 7))
+        rest = rest - parts[-1]
+    cut = jnp.concatenate(parts, axis=0).astype(bf16)
+    act_low = jnp.concatenate([act_all.reshape(-1, D)] * 3, axis=0).astype(bf16)
+    grad_w_ada = jnp.einsum("ld,lke->dke", act_low, cut, preferred_element_type=f32)
+    parts = []
+    rest = gmo[:6]
+    for _ in range(3):
+        parts.append(lax.reduce_precision(rest, 8, 7))
+        rest = rest - parts[-1]
+    own = jnp.stack(parts).astype(bf16)
     grad_silu = lax.psum(
-        jnp.einsum(
-            "ke,dke->d", gmo[:6], w_ada.astype(f32), precision=lax.Precision.HIGHEST,
-            preferred_element_type=f32,
-        )[None],
+        jnp.sum(
+            jnp.einsum("pke,dke->pd", own, w_ada, preferred_element_type=f32),
+            axis=0,
+            keepdims=True,
+        ),
         "col",
     )
     grad_cond = jax.vjp(jax.nn.silu, cond)[1](grad_silu)[0]

time: 253 us -> 248 us (0.980)
  matrix products: 13.9 us -> 9.04 us
    dot_general x2, matrix products: 11.5 us -> 6.62 us  [the longest x1 3.72 us: body(): jnp.einsum('ld,lke->dke', act_low, cut, preferred_element_type=f32)]
    unnamed x41 -> x42, local copies, waits for them, and re-layouts: 5.47 us -> 5.48 us
where the time goes in v3:
time: 248 us
  Pallas kernels  218 us (88%)
  matrix products  9.04 us (4%)
  other arithmetic  8.06 us (3%)
  local copies, waits for them, and re-layouts  6.09 us (2%)
  blocking collectives  5.95 us (2%)
    pallas_call x1, Pallas kernels, call_mega(): pl.pallas_call(functools.partial(mega, ndp), out_shape=[o[0] for o in out...  218 us
    psum x1, blocking collectives, body(): lax.psum(jnp.sum(jnp.einsum('pke,dke->pd', own, w_ada, preferred_element_...  5.95 us
    unnamed x42, local copies, waits for them, and re-layouts  5.48 us

profile of v3, /device:TPU:0, one launch (start us, length us, event | category | flops | bytes accessed | tf_op | source)
XLA Modules:
  0.0 247.8 jit_solution(18317250870610345667)
XLA Ops:
  0.7 1.3 convert_convert_fusion
  2.0 0.6 copy-done.8
  2.5 2.4 fusion.17
  5.0 0.6 concatenate.11.mod
  5.6 217.9 %block.1 = (f32[1024,256]{1,0:T(8,128)}, f32[1024,256]{1,0:T(8,128)}, bf16[3,256,512]{2,1,0:T(8,128)(2,1)}, bf16[512,256]{1,0:T(8,128)(2,1)}, bf16[256,2048]{1,0...) custom-call(f32[1024,256]{1,0:T(8,128)} %x_hbm.1, ...), custom_call_target="tpu_custom_call" | custom-call | tf_op jit(solution)/shard_map/block/pallas_call | solution.py:1149
  223.5 0.0 copy-start.7
  223.5 0.0 copy-start.9
  223.5 0.8 fusion.15
  224.4 0.0 copy-start.1
  224.4 2.9 %fusion = f32[1024]{0:T(1024)S(1)} fusion(bf16[1024,6,256]{2,0,1:T(8,128)(2,1)} %param.15, bf16[3,6,256]{2,1,0:T(8,128)(2,1)S(1)} %pad_maximum_fusion.1), kind=kOutput, calls=%fused_computation.1 | convolution fusion | flops 9439232 | bytes 3159040 | tf_op jit(solution)/shard_map/pke,dke->pd/dot_general | solution.py:1195
  227.3 5.9 %psum.7 = f32[1,1024]{1,0:T(1,128)S(1)} all-reduce(f32[1,1024]{1,0:T(1,128)S(1)} %bitcast.37), channel_id=1, replica_groups=mesh['dp'=4,'row'=2,'col'=4] {'col'}, use_global_device_ids=true, to_apply=%region_1.2 | all-reduce | flops 1024 | bytes 8192 | tf_op jit(solution)/shard_map/psum | solution.py:1193
  233.2 0.0 copy-done.9
  233.2 0.6 fusion.13
  233.9 0.0 copy-done.5
  233.9 0.0 copy-start
  233.9 0.8 convert_element_type.24
  234.8 1.4 convert_element_type.23
  236.1 1.6 convert_element_type.25
  237.7 0.0 copy-done
  237.7 1.5 bitcast_convert_fusion
  239.2 3.7 %fusion.1 = f32[1024,6,256]{2,0,1:T(8,128)} fusion(bf16[24,6,256]{2,1,0:T(8,128)(2,1)S(1)} %pad_maximum_fusion, bf16[8,1024]{1,0:T(8,128)(2,1)S(1)} %bitcast.36), kind=kOutput, calls=%fused_computation.8 | convolution fusion | flops 75644928 | bytes 6381568 | tf_op jit(solution)/shard_map/ld,lke->dke/dot_general | solution.py:1186
  243.0 1.0 copy.44
  244.0 0.0 copy-done.2
  244.0 1.0 copy.45
  244.9 0.0 copy-done.11
  244.9 0.6 copy.46
  245.5 0.0 copy-done.16
  245.5 0.6 copy.47
  246.1 0.0 copy-done.15
  246.1 0.6 copy.48
  246.7 0.6 copy.49
  247.3 0.6 copy.50
  (28 shorter events, 0.1 us)
Async XLA Ops:
  0.6 4.3 %copy-start.12 = (f32[6,256]{1,0:T(8,128)S(1)}, f32[6,256]{1,0:T(8,128)}, u32[]{:S(2)}) copy-start(f32[6,256]{1,0:T(8,128)} %param.16) | copy-start | bytes 18436
  2.0 0.6 copy-start.8
  223.5 9.7 %copy-start.7 = (f32[1,1024]{1,0:T(1,128)S(1)}, f32[1,1024]{1,0:T(1,128)}, u32[]{:S(2)}) copy-start(f32[1,1024]{1,0:T(1,128)} %param.14) | copy-start | bytes 12292
  223.5 9.7 %copy-start.9 = (f32[1,1024]{1,0:T(1,128)S(1)}, f32[1,1024]{1,0:T(1,128)}, u32[]{:S(2)}) copy-start(f32[1,1024]{1,0:T(1,128)} %copy-done.8) | copy-start | bytes 12292
  223.5 10.3 %copy-start.10 = (f32[8,8,128]{2,1,0:T(8,128)S(1)}, f32[8,8,128]{2,1,0:T(8,128)}, u32[]{:S(2)}) copy-start(f32[8,8,128]{2,1,0:T(8,128)} %get-tuple-element.30) | copy-start | bytes 98308
  223.5 10.3 %copy-start.6 = (f32[8,8,256]{2,1,0:T(8,128)S(1)}, f32[8,8,256]{2,1,0:T(8,128)}, u32[]{:S(2)}) copy-start(f32[8,8,256]{2,1,0:T(8,128)} %get-tuple-element.31) | copy-start | bytes 196612
  223.5 10.4 %copy-start.5 = (bf16[512,256]{1,0:T(8,128)(2,1)S(1)}, bf16[512,256]{1,0:T(8,128)(2,1)}, u32[]{:S(2)}) copy-start(bf16[512,256]{1,0:T(8,128)(2,1)} %get-tuple-element.35) | copy-start | bytes 786436
  223.5 11.2 %copy-start.4 = (bf16[3,256,512]{2,1,0:T(8,128)(2,1)S(1)}, bf16[3,256,512]{2,1,0:T(8,128)(2,1)}, u32[]{:S(2)}) copy-start(bf16[3,256,512]{2,1,0:T(8,128)(2,1)} %get-tuple-element.33) | copy-start | bytes 2359300
  224.4 11.8 %copy-start.1 = (bf16[256,2048]{1,0:T(8,128)(2,1)S(1)}, bf16[256,2048]{1,0:T(8,128)(2,1)}, u32[]{:S(2)}) copy-start(bf16[256,2048]{1,0:T(8,128)(2,1)} %get-tuple-element.37) | copy-start | bytes 3145732
  233.9 3.8 %copy-start = (bf16[4,512,256]{2,1,0:T(8,128)(2,1)S(1)}, bf16[4,512,256]{2,1,0:T(8,128)(2,1)}, u32[]{:S(2)}) copy-start(bf16[4,512,256]{2,1,0:T(8,128)(2,1)} %get-tuple-element.39) | copy-start | bytes 3145732
  239.2 3.7 %copy-start.3 = (f32[1024,256]{1,0:T(8,128)S(1)}, f32[1024,256]{1,0:T(8,128)}, u32[]{:S(2)}) copy-start(f32[1024,256]{1,0:T(8,128)} %get-tuple-element.62) | copy-start | bytes 3145732
  239.2 4.7 %copy-start.2 = (f32[1024,256]{1,0:T(8,128)S(1)}, f32[1024,256]{1,0:T(8,128)}, u32[]{:S(2)}) copy-start(f32[1024,256]{1,0:T(8,128)} %get-tuple-element.63) | copy-start | bytes 3145732
  243.0 2.0 copy-start.11
  243.0 2.6 %copy-start.16 = (f32[2,128]{1,0:T(2,128)S(1)}, f32[2,128]{1,0:T(2,128)}, u32[]{:S(2)}) copy-start(f32[2,128]{1,0:T(2,128)} %get-tuple-element.68) | copy-start | bytes 3076
  243.0 3.1 %copy-start.15 = (f32[1,256]{1,0:T(1,128)S(1)}, f32[1,256]{1,0:T(1,128)}, u32[]{:S(2)}) copy-start(f32[1,256]{1,0:T(1,128)} %get-tuple-element.36) | copy-start | bytes 3076
  243.0 3.7 %copy-start.13 = (f32[1,512]{1,0:T(1,128)S(1)}, f32[1,512]{1,0:T(1,128)}, u32[]{:S(2)}) copy-start(f32[1,512]{1,0:T(1,128)} %get-tuple-element.38) | copy-start | bytes 6148
  243.0 4.3 %copy-start.14 = (f32[1,256]{1,0:T(1,128)S(1)}, f32[1,256]{1,0:T(1,128)}, u32[]{:S(2)}) copy-start(f32[1,256]{1,0:T(1,128)} %get-tuple-element.40) | copy-start | bytes 3076

commit v4 on v3

--- a/solution.py
+++ b/solution.py
@@ -24,10 +24,10 @@
     (100, 110, 121, 125.5),
     (107.5, 117.5, 125.5, 131.5),
     (112.5, 121, 131.5, 136),
-    (117.5, 128.5, 138, 149),
-    (122.5, 131.5, 139.5, 150),
-    (128.5, 138, 147, 152),
-    (136, 144, 153, 156),
+    (117.5, 128.5, 148, 152),
+    (122.5, 131.5, 148, 153),
+    (128.5, 138, 148, 154),
+    (136, 144, 153, 157),
     (138, 147, 155, 156),
     (142.5, 151, 159, 162),
     (147, 156, 164, 167),
@@ -1028,6 +1028,7 @@
         b1_sums(i)
         tick(142.5 + 1.5 * i)
     st4.exchange()
+    tick(148)
     phase("p50_b1stat")
     s1, s2 = st4.total()
     CV[6] = s1 / D
@@ -1044,16 +1045,16 @@
     put_grad.start()
     finals.append(put_grad.wait)
     tick(151)
+    tick(168)
     phase("p51_rsout")
     rs_mix.drain()
     loop(4, rs_out.one)
     loop(4, rs_out.two)
+    tick(1000)
+    phase("p51_out")
     loop(4, rs_out.three)
-    tick(153)
-    tick(156)
     for i in range(4):
         out_done(i)
-        tick(158 + 2.5 * i)
     put_result = lc(X, res_o, lsem())
     put_result.start()
     finals.append(put_result.wait)

time: 248 us -> 246 us (level)
  Pallas kernels: 218 us -> 215 us
where the time goes in v4:
time: 246 us
  Pallas kernels  215 us (87%)
  matrix products  9.04 us (4%)
  other arithmetic  8.06 us (3%)
  local copies, waits for them, and re-layouts  6.09 us (2%)
  blocking collectives  6.09 us (2%)
    pallas_call x1, Pallas kernels, call_mega(): pl.pallas_call(functools.partial(mega, ndp), out_shape=[o[0] for o in out...  215 us
    psum x1, blocking collectives, body(): lax.psum(jnp.sum(jnp.einsum('pke,dke->pd', own, w_ada, preferred_element_...  6.09 us
    unnamed x42, local copies, waits for them, and re-layouts  5.48 us

profile of v4, /device:TPU:0, one launch (start us, length us, event | category | flops | bytes accessed | tf_op | source)
XLA Modules:
  0.0 245.6 jit_solution(7110250051527278700)
XLA Ops:
  0.6 0.0 copy-start.12
  0.7 1.3 convert_convert_fusion
  2.0 0.6 copy-done.8
  2.5 2.4 fusion.17
  5.0 0.0 copy-done.12
  5.0 0.6 concatenate.11.mod
  5.6 215.5 %block.1 = (f32[1024,256]{1,0:T(8,128)}, f32[1024,256]{1,0:T(8,128)}, bf16[3,256,512]{2,1,0:T(8,128)(2,1)}, bf16[512,256]{1,0:T(8,128)(2,1)}, bf16[256,2048]{1,0...) custom-call(f32[1024,256]{1,0:T(8,128)} %x_hbm.1, ...), custom_call_target="tpu_custom_call" | custom-call | tf_op jit(solution)/shard_map/block/pallas_call | solution.py:1150
  221.1 0.0 copy-start.7
  221.1 0.0 copy-start.9
  221.1 0.0 copy-start.10
  221.1 0.0 copy-start.6
  221.1 0.0 copy-start.5
  221.1 0.8 fusion.15
  222.0 2.9 %fusion = f32[1024]{0:T(1024)S(1)} fusion(bf16[1024,6,256]{2,0,1:T(8,128)(2,1)} %param.15, bf16[3,6,256]{2,1,0:T(8,128)(2,1)S(1)} %pad_maximum_fusion.1), kind=kOutput, calls=%fused_computation.1 | convolution fusion | flops 9439232 | bytes 3159040 | tf_op jit(solution)/shard_map/pke,dke->pd/dot_general | solution.py:1196
  224.9 6.1 %psum.7 = f32[1,1024]{1,0:T(1,128)S(1)} all-reduce(f32[1,1024]{1,0:T(1,128)S(1)} %bitcast.37), channel_id=1, replica_groups=mesh['dp'=4,'row'=2,'col'=4] {'col'}, use_global_device_ids=true, to_apply=%region_1.2 | all-reduce | flops 1024 | bytes 8192 | tf_op jit(solution)/shard_map/psum | solution.py:1194
  231.0 0.0 copy-done.9
  231.0 0.6 fusion.13
  231.7 0.0 copy-done.5
  231.7 0.0 copy-start
  231.7 0.8 convert_element_type.24
  232.5 1.4 convert_element_type.23
  233.9 1.6 convert_element_type.25
  235.4 0.0 copy-done
  235.4 1.5 bitcast_convert_fusion
  237.0 3.7 %fusion.1 = f32[1024,6,256]{2,0,1:T(8,128)} fusion(bf16[24,6,256]{2,1,0:T(8,128)(2,1)S(1)} %pad_maximum_fusion, bf16[8,1024]{1,0:T(8,128)(2,1)S(1)} %bitcast.36), kind=kOutput, calls=%fused_computation.8 | convolution fusion | flops 75644928 | bytes 6381568 | tf_op jit(solution)/shard_map/ld,lke->dke/dot_general | solution.py:1187
  240.7 1.0 copy.44
  241.7 1.0 copy.45
  242.7 0.6 copy.46
  243.3 0.6 copy.47
  243.8 0.6 copy.48
  244.4 0.6 copy.49
  245.0 0.6 copy.50
  (28 shorter events, 0.1 us)
Async XLA Ops:
  0.6 4.3 %copy-start.12 = (f32[6,256]{1,0:T(8,128)S(1)}, f32[6,256]{1,0:T(8,128)}, u32[]{:S(2)}) copy-start(f32[6,256]{1,0:T(8,128)} %param.16) | copy-start | bytes 18436
  2.0 0.6 copy-start.8
  221.1 9.9 %copy-start.7 = (f32[1,1024]{1,0:T(1,128)S(1)}, f32[1,1024]{1,0:T(1,128)}, u32[]{:S(2)}) copy-start(f32[1,1024]{1,0:T(1,128)} %param.14) | copy-start | bytes 12292
  221.1 9.9 %copy-start.9 = (f32[1,1024]{1,0:T(1,128)S(1)}, f32[1,1024]{1,0:T(1,128)}, u32[]{:S(2)}) copy-start(f32[1,1024]{1,0:T(1,128)} %copy-done.8) | copy-start | bytes 12292
  221.1 10.5 %copy-start.10 = (f32[8,8,128]{2,1,0:T(8,128)S(1)}, f32[8,8,128]{2,1,0:T(8,128)}, u32[]{:S(2)}) copy-start(f32[8,8,128]{2,1,0:T(8,128)} %get-tuple-element.30) | copy-start | bytes 98308
  221.1 10.5 %copy-start.6 = (f32[8,8,256]{2,1,0:T(8,128)S(1)}, f32[8,8,256]{2,1,0:T(8,128)}, u32[]{:S(2)}) copy-start(f32[8,8,256]{2,1,0:T(8,128)} %get-tuple-element.31) | copy-start | bytes 196612
  221.1 10.5 %copy-start.5 = (bf16[512,256]{1,0:T(8,128)(2,1)S(1)}, bf16[512,256]{1,0:T(8,128)(2,1)}, u32[]{:S(2)}) copy-start(bf16[512,256]{1,0:T(8,128)(2,1)} %get-tuple-element.35) | copy-start | bytes 786436
  221.1 11.4 %copy-start.4 = (bf16[3,256,512]{2,1,0:T(8,128)(2,1)S(1)}, bf16[3,256,512]{2,1,0:T(8,128)(2,1)}, u32[]{:S(2)}) copy-start(bf16[3,256,512]{2,1,0:T(8,128)(2,1)} %get-tuple-element.33) | copy-start | bytes 2359300
  221.9 11.9 %copy-start.1 = (bf16[256,2048]{1,0:T(8,128)(2,1)S(1)}, bf16[256,2048]{1,0:T(8,128)(2,1)}, u32[]{:S(2)}) copy-start(bf16[256,2048]{1,0:T(8,128)(2,1)} %get-tuple-element.37) | copy-start | bytes 3145732
  231.7 3.8 %copy-start = (bf16[4,512,256]{2,1,0:T(8,128)(2,1)S(1)}, bf16[4,512,256]{2,1,0:T(8,128)(2,1)}, u32[]{:S(2)}) copy-start(bf16[4,512,256]{2,1,0:T(8,128)(2,1)} %get-tuple-element.39) | copy-start | bytes 3145732
  237.0 3.7 %copy-start.3 = (f32[1024,256]{1,0:T(8,128)S(1)}, f32[1024,256]{1,0:T(8,128)}, u32[]{:S(2)}) copy-start(f32[1024,256]{1,0:T(8,128)} %get-tuple-element.62) | copy-start | bytes 3145732
  237.0 4.7 %copy-start.2 = (f32[1024,256]{1,0:T(8,128)S(1)}, f32[1024,256]{1,0:T(8,128)}, u32[]{:S(2)}) copy-start(f32[1024,256]{1,0:T(8,128)} %get-tuple-element.63) | copy-start | bytes 3145732
  240.7 2.0 copy-start.11
  240.7 2.6 %copy-start.16 = (f32[2,128]{1,0:T(2,128)S(1)}, f32[2,128]{1,0:T(2,128)}, u32[]{:S(2)}) copy-start(f32[2,128]{1,0:T(2,128)} %get-tuple-element.68) | copy-start | bytes 3076
  240.7 3.1 %copy-start.15 = (f32[1,256]{1,0:T(1,128)S(1)}, f32[1,256]{1,0:T(1,128)}, u32[]{:S(2)}) copy-start(f32[1,256]{1,0:T(1,128)} %get-tuple-element.36) | copy-start | bytes 3076
  240.7 3.7 %copy-start.13 = (f32[1,512]{1,0:T(1,128)S(1)}, f32[1,512]{1,0:T(1,128)}, u32[]{:S(2)}) copy-start(f32[1,512]{1,0:T(1,128)} %get-tuple-element.38) | copy-start | bytes 6148
  240.7 4.3 %copy-start.14 = (f32[1,256]{1,0:T(1,128)S(1)}, f32[1,256]{1,0:T(1,128)}, u32[]{:S(2)}) copy-start(f32[1,256]{1,0:T(1,128)} %get-tuple-element.40) | copy-start | bytes 3076
